TPU v7x, 256 devices: a 8x8x2 block of a 8x8x16 slice. The times are simulated.
256 devices in a mesh: groups: 2 (over z), seq: 16 (over y, core), head: 8 (over x).
Axes of the slice: x: 8, y: 8, z: 2, core: 2. Of those that a mesh axis runs over, the one named last changes fastest.
The devices are a block of a 8x8x16 slice.
Arguments:
- query: bfloat16 [32, 16, 1024], P('groups', None, 'head'), parts along dimension 0, may hold values from -6 to 6, as said below
- new_key: bfloat16 [32, 16, 1024], P('groups', None, 'head'), parts along dimension 0, may hold values from -6 to 6
- new_value: bfloat16 [32, 16, 1024], P('groups', None, 'head'), parts along dimension 0, may hold values from -6 to 6
- keys: bfloat16 [32, 16384, 1024], P('groups', 'seq', 'head'), parts along dimension 0, may hold values from -6 to 6, as said below
- values: bfloat16 [32, 16384, 1024], P('groups', 'seq', 'head'), parts along dimension 0, may hold values from -6 to 6
- lengths: int32 [32], P('groups'), parts along dimension 0, may hold values from 2 to 16384
- time_bucket: int32 [32, 16384], P('groups', 'seq'), parts along dimension 0, may hold values from 0 to 63
- action: int32 [32, 16384], P('groups', 'seq'), parts along dimension 0, may hold values from 0 to 15
- time_bias: float32 [64, 8], P(None, 'head'), may hold values from -0.25 to 0.25
- action_bias: float32 [16, 8], P(None, 'head'), may hold values from -0.25 to 0.25
- gate: bfloat16 [32, 16, 1024], P('groups', None, 'head'), parts along dimension 0, may hold values from -6 to 6
- norm_gain: float32 [1024], P('head'), may hold values from 0.1 to 1.9
- w_out: bfloat16 [1024, 1024], P('head'), may hold values from -0.1875 to 0.1875
Outputs:
- output: bfloat16 [32, 16, 1024], P(('groups', 'seq'), None, 'head'), parts along dimension 0
There are 2 independent parts, one for each index of `groups`. A program takes and returns all parts, laid end to end along the dimension named above; an argument that names none is the same for every part. Nothing has to cross between parts.
Inputs may be any that keep to these rules, and one draw needn't show every extreme that they name: `query`: queries of order one; some users' queries may be large and equal to some of their keys. `keys`: keys of order one.
All inputs are finite; a program needn't handle non-finite values.
Results may differ from a plain program's by a relative error of at most 0.0056.
Values sent between devices are 32-bit elements; how exact they have to be, the bound alone decides.
A program may use at most 64 MiB of HBM per device.

v0:
```python
import math

import jax
import jax.numpy as jnp
from jax import lax
from jax.sharding import PartitionSpec as P


def sent_together(arrays, axis, split_dim, concat_dim, along):
    widths = [math.prod(a.shape[along:]) for a in arrays]
    both = jnp.concatenate(
        [a.reshape(*a.shape[:along], w) for a, w in zip(arrays, widths)], axis=along
    )
    whole = lax.all_to_all(both, axis, split_axis=split_dim, concat_axis=concat_dim, tiled=True)
    blocks = jnp.split(whole, [sum(widths[:k]) for k in range(1, len(widths))], axis=along)
    return tuple(
        (b.reshape(*whole.shape[:along], *a.shape[along:]) for a, b in zip(arrays, blocks))
    )


def sent_to_all(shard, axis):
    count = lax.axis_size(axis)
    return lax.all_to_all(
        jnp.broadcast_to(shard[None], (count, *shard.shape)), axis, 0, 0, tiled=True
    )


def over_copies(shard, axis):
    return sent_to_all(shard, axis).sum(axis=0)


def cut_along(shard, dim, count):
    before, after = (shard.shape[:dim], shard.shape[dim + 1 :])
    return jnp.moveaxis(shard.reshape(*before, count, -1, *after), dim, 0)


def sent_and_summed(shard, axis, dim):
    blocks = cut_along(shard, dim, lax.axis_size(axis))
    arrived = lax.all_to_all(blocks, axis, split_axis=0, concat_axis=0, tiled=True)
    return arrived.sum(axis=0)


def body(
    query,
    new_key,
    new_value,
    keys,
    values,
    lengths,
    time_bucket,
    action,
    time_bias,
    action_bias,
    gate,
    norm_gain,
    w_out,
):
    user_count, block_len, row_width = keys.shape
    cand_count = query.shape[1]
    head_count = time_bias.shape[1]
    head_size = row_width // head_count
    score_scale = 1.0 / math.sqrt(head_size)
    seq_count = lax.axis_size("seq")
    seq_rank = lax.axis_index("seq")
    query_heads = query.reshape(user_count, cand_count, head_count, head_size)
    key_heads = keys.reshape(user_count, block_len, head_count, head_size)
    value_heads = values.reshape(user_count, block_len, head_count, head_size)
    scores = (
        jnp.einsum("uchd,ushd->uchs", query_heads, key_heads, preferred_element_type=jnp.float32)
        * score_scale
    )
    bucket_onehot = (
        time_bucket[:, :, None] == jnp.arange(time_bias.shape[0], dtype=jnp.int32)[None, None, :]
    ).astype(jnp.float32)
    action_onehot = (
        action[:, :, None] == jnp.arange(action_bias.shape[0], dtype=jnp.int32)[None, None, :]
    ).astype(jnp.float32)
    biases = jnp.einsum("usb,bh->uhs", bucket_onehot, time_bias, precision=lax.Precision.HIGHEST)
    biases = biases + jnp.einsum(
        "usb,bh->uhs", action_onehot, action_bias, precision=lax.Precision.HIGHEST
    )
    scores = scores + biases[:, None]
    position = seq_rank * block_len + jnp.arange(block_len, dtype=jnp.int32)
    valid = position[None, None, None, :] < lengths[:, None, None, None]
    block_max = jnp.max(jnp.where(valid, scores, -1e30), axis=-1)
    weights = jnp.where(valid, jnp.exp(scores - block_max[..., None]), 0.0)
    block_sum = jnp.sum(weights, axis=-1)
    block_acc = jnp.einsum(
        "uchs,ushd->uchd",
        weights.astype(jnp.bfloat16),
        value_heads,
        preferred_element_type=jnp.float32,
    )
    local_users = user_count // seq_count
    first_user = seq_rank * local_users

    def own_rows(source):
        return lax.dynamic_slice_in_dim(source, first_user, local_users, 0)

    received = sent_together((block_max[None], block_sum[None], block_acc[None]), "seq", 1, 0, 4)
    running_max = jnp.max(received[0], axis=0)
    factors = jnp.exp(received[0] - running_max[None])
    total = jnp.sum(factors * received[1], axis=0)
    accum = jnp.sum(factors[..., None] * received[2], axis=0)
    own_query = (
        own_rows(query).astype(jnp.float32).reshape(local_users, cand_count, head_count, head_size)
    )
    own_key = (
        own_rows(new_key)
        .astype(jnp.float32)
        .reshape(local_users, cand_count, head_count, head_size)
    )
    own_value = (
        own_rows(new_value)
        .astype(jnp.float32)
        .reshape(local_users, cand_count, head_count, head_size)
    )
    own_score = jnp.sum(own_query * own_key, axis=-1) * score_scale
    overall = jnp.maximum(running_max, own_score)
    past_factor = jnp.exp(running_max - overall)
    own_factor = jnp.exp(own_score - overall)
    attended = (past_factor[..., None] * accum + own_factor[..., None] * own_value) / (
        past_factor * total + own_factor
    )[..., None]
    local_squares = jnp.sum(jnp.square(attended), axis=(2, 3))
    full_width = row_width * lax.axis_size("head")
    gate_heads = (
        own_rows(gate).astype(jnp.float32).reshape(local_users, cand_count, head_count, head_size)
    )
    hidden = (attended * norm_gain.reshape(head_count, head_size) * jax.nn.silu(gate_heads)).astype(
        jnp.bfloat16
    )
    hidden = hidden.reshape(local_users * cand_count, row_width)
    partial_out = jnp.dot(hidden, w_out, preferred_element_type=jnp.float32).reshape(
        local_users, cand_count, -1
    )
    squares = over_copies(local_squares, "head")
    projected = sent_and_summed(partial_out, "head", 2)
    factor = 1.0 / jnp.sqrt(squares / full_width + 1e-06)
    return (projected * factor[:, :, None]).astype(jnp.bfloat16)


def solution(mesh):
    placed = (
        P("groups", None, "head"),
        P("groups", None, "head"),
        P("groups", None, "head"),
        P("groups", "seq", "head"),
        P("groups", "seq", "head"),
        P("groups"),
        P("groups", "seq"),
        P("groups", "seq"),
        P(None, "head"),
        P(None, "head"),
        P("groups", None, "head"),
        P("head"),
        P("head", None),
    )
    return jax.shard_map(
        body,
        mesh=mesh,
        in_specs=placed,
        out_specs=P(("groups", "seq"), None, "head"),
        check_vma=False,
    )
```

profile of v0, /device:TPU:513, one launch (start us, length us, event | category | flops | bytes accessed | tf_op | source)
XLA Modules:
  0.0 71.6 jit_solution(11396828265111893377)
XLA Ops:
  0.0 0.0 copy-start
  0.0 0.7 %broadcast_compare_fusion = pred[16,1024]{1,0:T(8,128)(4,1)S(1)} fusion(s32[1024]{0:T(1024)S(1)} %iota_add_fusion, s32[16]{0:T(128)} %param.18), kind=kLoop, calls=%fused_computation.23 | loop fusion | flops 16384 | bytes 20544 | tf_op jit(solution)/shard_map/lt | solution.py:84
  0.8 0.0 copy-done
  0.8 2.2 %fusion = f32[1,16,1024]{2,0,1:T(1,128)S(1)} fusion(s32[16,1024]{1,0:T(8,128)} %param.19, f32[64,1]{0,1:T(1,128)S(1)} %copy-done), kind=kOutput, calls=%fused_computation.1 | convolution fusion | flops 13631488 | bytes 131328 | tf_op jit(solution)/shard_map/usb,bh->uhs/dot_general | solution.py:78
  3.0 1.3 %fusion.5 = f32[1,16,1024]{2,0,1:T(1,128)S(1)} fusion(s32[16,1024]{1,0:T(8,128)} %param.20, f32[16,1]{0,1:T(1,128)} %param.22), kind=kOutput, calls=%fused_computation.15 | convolution fusion | flops 3407872 | bytes 131136 | tf_op jit(solution)/shard_map/usb,bh->uhs/dot_general | solution.py:79
  4.3 3.5 %select_reduce_fusion = (f32[16,16]{1,0:T(8,128)S(1)}, f32[16,1,1024,16]{2,3,0,1:T(8,128)S(1)}) fusion(pred[16,1024]{1,0:T(8,128)(4,1)S(1)} %broadcast_compare_fusion, f32[16,1024]{1,0:T(8,128)S(1)} %bitcast_add_fusion, bf16[16,1024,128]{2,1,0:T(8,128)(2,1)} %param.16, bf16[16,16,128]{2,1,0:T(8,128)(2,1)} %param.13), kind=kOutput, calls=%fused_computation.13 | convolution fusion | flops 68157184 | bytes 5391360 | tf_op jit(solution)/shard_map/uchd,ushd->uchs/dot_general | solution.py:69
  7.8 0.0 copy-start.1
  7.8 0.4 bitcast_reduce_fusion
  8.1 0.2 copy.67
  8.3 0.0 copy-start.2
  8.3 3.0 %convolution_bitcast_fusion = f32[1,16,16,1,128]{4,2,1,3,0:T(8,128)S(1)} fusion(bf16[16,1024,128]{2,1,0:T(8,128)(2,1)} %param.17, f32[16,1,1024,16]{2,3,0,1:T(8,128)S(1)} %get-tuple-element.9, f32[16,16]{1,0:T(8,128)S(1)} %get-tuple-element.8, pred[16,1024]{1,0:T(8,128)(4,1)S(1)} %broadcast_compare_fusion), kind=kOutput, calls=%fused_computation.6 | convolution fusion | flops 67895296 | bytes 5391360 | tf_op jit(solution)/shard_map/uchs,ushd->uchd/dot_general | solution.py:88
  11.3 0.2 copy.66
  11.5 0.9 %maximum_bitcast_fusion = f32[1,16,16,1,130]{4,2,3,0,1:T(8,128)} fusion(f32[1,16,16,1,128]{4,2,1,3,0:T(8,128)S(1)} %convolution_bitcast_fusion, f32[1,16,16,1,1]{4,2,1,3,0:T(8,128)S(1)} %copy.67, f32[1,16,16,1,1]{4,2,1,3,0:T(8,128)S(1)} %copy.66), kind=kLoop, calls=%fused_computation.21 | loop fusion | flops 66560 | bytes 266240 | tf_op jit(solution)/shard_map/concatenate | solution.py:11
  12.4 23.7 %all-to-all-start = ((f32[1,16,16,1,130]{4,2,3,0,1:T(8,128)}), f32[1,16,16,1,130]{4,2,3,0,1:T(8,128)S(1)}, u32[]{:S(2)}, u32[]{:S(2)}) async-start(f32[1,16,16,1,130]{4,2,3,0,1:T(8,128)} %maximum_bitcast_fusion), calls=%async_computation | async-start | bytes 524288 | tf_op jit(solution)/shard_map/all_to_all | solution.py:14
  36.1 0.0 copy-done.1
  36.1 0.2 copy.77
  36.3 0.8 %multiply_reduce_fusion = f32[16]{0:T(128)S(1)} fusion(bf16[16,16,128]{2,1,0:T(8,128)(2,1)} %param.14, s32[]{:T(128)S(6)} %select_n.16, bf16[16,16,128]{2,1,0:T(8,128)(2,1)} %param.13), kind=kLoop, calls=%fused_computation.49 | loop fusion | flops 8176 | bytes 8260 | tf_op jit(solution)/shard_map/reduce_sum | solution.py:118
  37.1 11.0 %all-to-all-done = f32[1,16,16,1,130]{4,2,3,0,1:T(8,128)S(1)} async-done(((f32[1,16,16,1,130]{4,2,3,0,1:T(8,128)}), f32[1,16,16,1,130]{4,2,3,0,1:T(8,128)S(1)}, u32[]{:S(2)}, u32[]{:S(2)}) %all-to-all-start) | async-done | bytes 133152 | tf_op jit(solution)/shard_map/all_to_all | solution.py:14
  48.1 0.7 %copy.69 = f32[1,16,16,1,130]{2,1,4,3,0:T(8,128)S(1)} copy(f32[1,16,16,1,130]{4,2,3,0,1:T(8,128)S(1)} %all-to-all-done) | data formatting | bytes 266240 | tf_op jit(solution)/shard_map/all_to_all | solution.py:14
  48.9 0.2 fusion.4
  49.1 0.1 copy.70
  49.2 0.9 %fusion.27 = f32[16]{0:T(128)S(1)} fusion(f32[16,128]{1,0:T(8,128)S(1)} %copy.70, f32[16]{0:T(128)S(1)} %get-tuple-element.5, f32[16]{0:T(128)S(1)} %get-tuple-element.7, f32[16]{0:T(128)S(1)} %get-tuple-element.6, bf16[16,16,128]{2,1,0:T(8,128)(2,1)} %param.15, s32[]{:T(128)S(6)} %select_n.16), kind=kLoop, calls=%fused_computation.50 | loop fusion | flops 14320 | bytes 12548 | tf_op jit(solution)/shard_map/reduce_sum | solution.py:125
  50.1 0.6 broadcast_in_dim.48
  50.7 3.5 %all-to-all-start.2 = ((f32[8,1,16]{2,1,0:T(1,128)}), f32[8,1,16]{2,1,0:T(1,128)S(1)}, u32[]{:S(2)}, u32[]{:S(2)}) async-start(f32[8,1,16]{2,1,0:T(1,128)} %broadcast_in_dim.48), calls=%async_computation.2 | async-start | bytes 8192 | tf_op jit(solution)/shard_map/all_to_all | solution.py:23
  54.2 0.0 copy-done.2
  54.2 1.6 %convolution_bitcast_fusion.1 = f32[8,1,16,128]{3,2,1,0:T(8,128)} fusion(bf16[8,128,128]{2,1,0:T(8,128)(2,1)S(1)} %bitcast.107, f32[16,128]{1,0:T(8,128)S(1)} %copy.70, bf16[16,16,128]{2,1,0:T(8,128)(2,1)} %param.23, s32[]{:T(128)S(6)} %select_n.16, f32[128]{0:T(128)S(1)} %copy-done.2, f32[16]{0:T(128)S(1)} %get-tuple-element.5, ...), kind=kOutput, calls=%fused_computation.7 | convolution fusion | flops 4220928 | bytes 344772 | tf_op jit(solution)/shard_map/dot_general | solution.py:134
  55.8 4.7 %all-to-all-done.2 = f32[8,1,16]{2,1,0:T(1,128)S(1)} async-done(((f32[8,1,16]{2,1,0:T(1,128)}), f32[8,1,16]{2,1,0:T(1,128)S(1)}, u32[]{:S(2)}, u32[]{:S(2)}) %all-to-all-start.2) | async-done | bytes 544 | tf_op jit(solution)/shard_map/all_to_all | solution.py:23
  60.5 3.6 %all-to-all-start.1 = ((f32[8,1,16,128]{3,2,1,0:T(8,128)}), f32[8,1,16,128]{3,2,1,0:T(8,128)S(1)}, u32[]{:S(2)}, u32[]{:S(2)}) async-start(f32[8,1,16,128]{3,2,1,0:T(8,128)} %convolution_bitcast_fusion.1), calls=%async_computation.1 | async-start | bytes 131072 | tf_op jit(solution)/shard_map/all_to_all | solution.py:39
  64.0 6.8 %all-to-all-done.1 = f32[8,1,16,128]{3,2,1,0:T(8,128)S(1)} async-done(((f32[8,1,16,128]{3,2,1,0:T(8,128)}), f32[8,1,16,128]{3,2,1,0:T(8,128)S(1)}, u32[]{:S(2)}, u32[]{:S(2)}) %all-to-all-start.1) | async-done | bytes 65568 | tf_op jit(solution)/shard_map/all_to_all | solution.py:39
  70.9 0.7 fusion.25
  (9 shorter events, 0.1 us)
Async XLA Ops:
  0.0 0.8 %copy-start = (f32[64,1]{0,1:T(1,128)S(1)}, f32[64,1]{0,1:T(1,128)}, u32[]{:S(2)}) copy-start(f32[64,1]{0,1:T(1,128)} %param.21) | copy-start | bytes 772
  7.8 28.4 %copy-start.1 = (bf16[128,1024]{1,0:T(8,128)(2,1)S(1)}, bf16[128,1024]{1,0:T(8,128)(2,1)}, u32[]{:S(2)}) copy-start(bf16[128,1024]{1,0:T(8,128)(2,1)} %param.25) | copy-start | bytes 786436
  8.3 45.9 %copy-start.2 = (f32[128]{0:T(128)S(1)}, f32[128]{0:T(128)}, u32[]{:S(2)}) copy-start(f32[128]{0:T(128)} %param.24) | copy-start | bytes 1540
  12.4 35.7 %all-to-all-start = ((f32[1,16,16,1,130]{4,2,3,0,1:T(8,128)}), f32[1,16,16,1,130]{4,2,3,0,1:T(8,128)S(1)}, u32[]{:S(2)}, u32[]{:S(2)}) async-start(f32[1,16,16,1,130]{4,2,3,0,1:T(8,128)} %maximum_bitcast_fusion), calls=%async_computation | async-start | bytes 524288 | tf_op jit(solution)/shard_map/all_to_all | solution.py:14
  50.7 9.8 %all-to-all-start.2 = ((f32[8,1,16]{2,1,0:T(1,128)}), f32[8,1,16]{2,1,0:T(1,128)S(1)}, u32[]{:S(2)}, u32[]{:S(2)}) async-start(f32[8,1,16]{2,1,0:T(1,128)} %broadcast_in_dim.48), calls=%async_computation.2 | async-start | bytes 8192 | tf_op jit(solution)/shard_map/all_to_all | solution.py:23
  60.5 10.4 %all-to-all-start.1 = ((f32[8,1,16,128]{3,2,1,0:T(8,128)}), f32[8,1,16,128]{3,2,1,0:T(8,128)S(1)}, u32[]{:S(2)}, u32[]{:S(2)}) async-start(f32[8,1,16,128]{3,2,1,0:T(8,128)} %convolution_bitcast_fusion.1), calls=%async_computation.1 | async-start | bytes 131072 | tf_op jit(solution)/shard_map/all_to_all | solution.py:39
where the time goes:
time: 72.1 us; the launch traced here: 71.6 us
  starting transfers between devices  30.8 us (43%)
  waiting for transfers between devices  22.5 us (31%)
  matrix products  11.5 us (16%)
  other arithmetic  4.75 us (7%)
  local copies, waits for them, and re-layouts  1.92 us (3%)
    all_to_all x1, starting transfers between devices, sent_together(): lax.all_to_all(both, axis, split_axis=split_dim, concat_axis=concat_dim,...  23.7 us
    all_to_all x1, waiting for transfers between devices, sent_together(): lax.all_to_all(both, axis, split_axis=split_dim, concat_axis=concat_dim,...  11 us
    all_to_all x1, waiting for transfers between devices, sent_and_summed(): lax.all_to_all(blocks, axis, split_axis=0, concat_axis=0, tiled=True)  6.84 us
    all_to_all x1, waiting for transfers between devices, sent_to_all(): lax.all_to_all(jnp.broadcast_to(shard[None], (count, *shard.shape)), axis...  4.66 us
    all_to_all x1, starting transfers between devices, sent_and_summed(): lax.all_to_all(blocks, axis, split_axis=0, concat_axis=0, tiled=True)  3.55 us
    all_to_all x1, starting transfers between devices, sent_to_all(): lax.all_to_all(jnp.broadcast_to(shard[None], (count, *shard.shape)), axis...  3.52 us
    dot_general x1, matrix products, body(): jnp.einsum('uchd,ushd->uchs', query_heads, key_heads, preferred_element_t...  3.48 us
    dot_general x1, matrix products, body(): jnp.einsum('uchs,ushd->uchd', weights.astype(jnp.bfloat16), value_heads,...  2.98 us
  transfers between devices with their start and end apart: 3, of which 3 were waited for; matrix products, arithmetic and copies ran while one was open for 4% of the time, Pallas kernels for 0%

commit v1 on v0

v1 whole, which is shorter than its diff:
```python
import functools
import math

import jax
import jax.numpy as jnp
from jax import lax
from jax.experimental import pallas as pl
from jax.experimental.pallas import tpu as pltpu
from jax.sharding import PartitionSpec as P

MESH = pl.DeviceIdType.MESH
LOG2E = math.log2(math.e)
LANES = 128
GROUP = 4


def far_first(count):
    return sorted(range(count), key=lambda d: (-min(d, count - d), d))


def table_lookup(table, index):
    rows = jnp.broadcast_to(table, (8, table.shape[1]))
    if table.shape[1] < LANES:
        rows = jnp.concatenate(
            [rows, jnp.zeros((8, LANES - table.shape[1]), rows.dtype)], axis=1
        )
    blocks = []
    for r in range(0, index.shape[0], 8):
        blocks.append(
            jnp.concatenate(
                [
                    jnp.take_along_axis(rows, index[r : r + 8, c : c + LANES], axis=1)
                    for c in range(0, index.shape[1], LANES)
                ],
                axis=1,
            )
        )
    return jnp.concatenate(blocks, axis=0)


def kernel(
    query,
    new_key,
    new_value,
    keys,
    values,
    lengths,
    time_bucket,
    action,
    time_bias,
    action_bias,
    gate,
    norm_gain,
    w_out,
    out,
    q_buf,
    nk_buf,
    nv_buf,
    k_buf,
    v_buf,
    len_buf,
    tb_buf,
    ac_buf,
    tbias_buf,
    abias_buf,
    gate_buf,
    gain_buf,
    w_buf,
    bias_buf,
    send1,
    recv1,
    send2,
    recv2,
    in_sem,
    k_sem,
    v_sem,
    send_sem1,
    recv_sem1,
    send_sem2,
    recv_sem2,
):
    n_seq = lax.axis_size("seq")
    n_head = lax.axis_size("head")
    me = lax.axis_index("seq")
    my_head = lax.axis_index("head")
    users, cands, width = query.shape
    block_len = keys.shape[1]
    half = cands // 2
    scale = LOG2E / math.sqrt(width)
    order = far_first(n_seq)

    def seq_peer(d):
        return lax.rem(me + d, n_seq)

    def head_peer(e):
        return lax.rem(my_head + e, n_head)

    small = [
        (lengths, len_buf),
        (time_bias, tbias_buf),
        (action_bias, abias_buf),
        (time_bucket, tb_buf),
        (action, ac_buf),
        (query, q_buf),
        (new_key.at[me], nk_buf),
        (new_value.at[me], nv_buf),
        (gate.at[me], gate_buf),
        (norm_gain, gain_buf),
        (w_out, w_buf),
    ]
    loads = [
        pltpu.make_async_copy(src, dst, in_sem.at[i]) for i, (src, dst) in enumerate(small)
    ]
    k_loads, v_loads = {}, {}
    for d in order:
        user = seq_peer(d)
        k_loads[d] = pltpu.make_async_copy(keys.at[user], k_buf.at[d], k_sem.at[d])
        v_loads[d] = pltpu.make_async_copy(values.at[user], v_buf.at[d], v_sem.at[d])
    for load in loads[:6]:
        load.start()
    for d in order:
        k_loads[d].start()
        v_loads[d].start()
    for load in loads[6:]:
        load.start()

    barrier = pltpu.get_barrier_semaphore()
    for d in order[:-1]:
        pl.semaphore_signal(barrier, inc=1, device_id={"seq": seq_peer(d)}, device_id_type=MESH)
    for e in range(1, n_head):
        pl.semaphore_signal(barrier, inc=1, device_id={"head": head_peer(e)}, device_id_type=MESH)

    for load in loads[:6]:
        load.wait()
    biases = table_lookup(tbias_buf[...], tb_buf[...]) + table_lookup(abias_buf[...], ac_buf[...])
    row = lax.broadcasted_iota(jnp.int32, (users, block_len), 0)
    limit = jnp.zeros((users, block_len), jnp.int32)
    for u in range(users):
        limit = jnp.where(row == u, len_buf[u], limit)
    position = me * block_len + lax.broadcasted_iota(jnp.int32, (users, block_len), 1)
    bias_buf[...] = jnp.where(position < limit, biases * LOG2E, -1e30)

    lane = lax.broadcasted_iota(jnp.int32, (half, LANES), 1)

    def attend(d):
        user = seq_peer(d)
        scores = (
            lax.dot_general(
                q_buf[user],
                k_buf[d],
                (((1,), (1,)), ((), ())),
                preferred_element_type=jnp.float32,
            )
            * scale
            + bias_buf[pl.ds(user, 1), :]
        )
        top = jnp.max(scores, axis=1, keepdims=True)
        weights = jnp.exp2(scores - top)
        total = jnp.sum(weights, axis=1, keepdims=True)
        acc = jnp.dot(
            weights.astype(jnp.bfloat16), v_buf[d], preferred_element_type=jnp.float32
        )
        packed = jnp.where(
            lane < 32,
            top[:half],
            jnp.where(lane < 64, top[half:], jnp.where(lane < 96, total[:half], total[half:])),
        )
        return acc, packed

    sends = []
    for first in range(0, n_seq, GROUP):
        group = order[first : first + GROUP]
        for d in group:
            k_loads[d].wait()
            v_loads[d].wait()
        for d in group:
            acc, packed = attend(d)
            place = recv1 if d == 0 else send1
            place[d, 0:cands] = acc
            place[d, cands : cands + half] = packed
        if first == 0:
            pl.semaphore_wait(barrier, n_seq - 1 + n_head - 1)
        for d in group:
            if d:
                copy = pltpu.make_async_remote_copy(
                    src_ref=send1.at[d],
                    dst_ref=recv1.at[d],
                    send_sem=send_sem1.at[d],
                    recv_sem=recv_sem1.at[d],
                    device_id={"seq": seq_peer(d)},
                    device_id_type=MESH,
                )
                copy.start()
                sends.append(copy)

    for load in loads[6:]:
        load.wait()
    own_query = q_buf[me].astype(jnp.float32)
    own = jnp.sum(own_query * nk_buf[...].astype(jnp.float32), axis=1, keepdims=True) * scale
    own = jnp.where(lane < 32, own[:half], own[half:])
    gate_rows = gate_buf[...].astype(jnp.float32)
    gated = gain_buf[...] * (gate_rows / (1.0 + jnp.exp(-gate_rows)))
    own_value = nv_buf[...].astype(jnp.float32)

    for copy in sends:
        copy.wait_recv()
    marks = [recv1[d, cands : cands + half] for d in range(n_seq)]
    overall = own
    for mark in marks:
        overall = jnp.maximum(overall, mark)
    factor = jnp.exp2(own - overall)

    def spread(values):
        return jnp.concatenate(
            [
                jnp.broadcast_to(values[:, 0:1], (half, width)),
                jnp.broadcast_to(values[:, 32:33], (half, width)),
            ],
            axis=0,
        )

    denom = factor
    numer = spread(factor) * own_value
    for d, mark in enumerate(marks):
        factor = jnp.exp2(mark - overall)
        denom = denom + factor * pltpu.roll(mark, 64, 1)
        numer = numer + spread(factor) * recv1[d, 0:cands]
    attended = numer / spread(denom)
    squares = jnp.sum(attended * attended, axis=1, keepdims=True)
    hidden = (attended * gated).astype(jnp.bfloat16)
    squares = jnp.where(lane < 32, squares[:half], squares[half:])
    for h in range(n_head):
        send2[h, 0:cands] = jnp.dot(
            hidden, w_buf[:, h * width : (h + 1) * width], preferred_element_type=jnp.float32
        )
        send2[h, cands : cands + half] = squares
    sends2 = []
    for e in far_first(n_head)[:-1]:
        copy = pltpu.make_async_remote_copy(
            src_ref=send2.at[head_peer(e)],
            dst_ref=recv2.at[e],
            send_sem=send_sem2.at[e],
            recv_sem=recv_sem2.at[e],
            device_id={"head": head_peer(e)},
            device_id_type=MESH,
        )
        copy.start()
        sends2.append(copy)
    whole = send2[my_head]
    for copy in sends2:
        copy.wait_recv()
    for e in range(1, n_head):
        whole = whole + recv2[e]
    square_sum = spread(whole[cands : cands + half])
    scaled = whole[0:cands] * (1.0 / jnp.sqrt(square_sum / (width * n_head) + 1e-06))
    out[0] = scaled.astype(out.dtype)
    for copy in sends + sends2:
        copy.wait_send()


def body(
    query,
    new_key,
    new_value,
    keys,
    values,
    lengths,
    time_bucket,
    action,
    time_bias,
    action_bias,
    gate,
    norm_gain,
    w_out,
):
    users, block_len, width = keys.shape
    cands = query.shape[1]
    n_seq, n_head = lax.axis_size("seq"), lax.axis_size("head")
    assert users == n_seq and width == LANES and w_out.shape[1] == n_head * width
    tile = cands + cands // 2
    bf16, f32, i32 = jnp.bfloat16, jnp.float32, jnp.int32
    vmem, dma = pltpu.VMEM, pltpu.SemaphoreType.DMA
    buckets, actions = time_bias.shape[0], action_bias.shape[0]
    return pl.pallas_call(
        kernel,
        name="decode",
        out_shape=jax.ShapeDtypeStruct((users // n_seq, cands, width), bf16),
        in_specs=[pl.BlockSpec(memory_space=pl.ANY)] * 13,
        out_specs=pl.BlockSpec(memory_space=vmem),
        scratch_shapes=[
            vmem((users, cands, width), bf16),
            vmem((cands, width), bf16),
            vmem((cands, width), bf16),
            vmem((users, block_len, width), bf16),
            vmem((users, block_len, width), bf16),
            pltpu.SMEM((users,), i32),
            vmem((users, block_len), i32),
            vmem((users, block_len), i32),
            vmem((1, buckets), f32),
            vmem((1, actions), f32),
            vmem((cands, width), bf16),
            vmem((1, width), f32),
            vmem((width, n_head * width), bf16),
            vmem((users, block_len), f32),
            vmem((n_seq, tile, width), f32),
            vmem((n_seq, tile, width), f32),
            vmem((n_head, tile, width), f32),
            vmem((n_head, tile, width), f32),
            dma((11,)),
            dma((n_seq,)),
            dma((n_seq,)),
            dma((n_seq,)),
            dma((n_seq,)),
            dma((n_head,)),
            dma((n_head,)),
        ],
        compiler_params=pltpu.CompilerParams(collective_id=0, has_side_effects=True),
    )(
        query,
        new_key,
        new_value,
        keys,
        values,
        lengths,
        time_bucket,
        action,
        time_bias.reshape(1, buckets),
        action_bias.reshape(1, actions),
        gate,
        norm_gain.reshape(1, width),
        w_out,
    )


def solution(mesh):
    placed = (
        P("groups", None, "head"),
        P("groups", None, "head"),
        P("groups", None, "head"),
        P("groups", "seq", "head"),
        P("groups", "seq", "head"),
        P("groups"),
        P("groups", "seq"),
        P("groups", "seq"),
        P(None, "head"),
        P(None, "head"),
        P("groups", None, "head"),
        P("head"),
        P("head", None),
    )
    return jax.shard_map(
        body,
        mesh=mesh,
        in_specs=placed,
        out_specs=P(("groups", "seq"), None, "head"),
        check_vma=False,
    )
```

time: 72.1 us -> 36.3 us (0.50)
  Pallas kernels: 0 us -> 34.9 us
  starting transfers between devices: 30.8 us -> 0 us
  waiting for transfers between devices: 22.5 us -> 0 us
  matrix products: 11.5 us -> 0 us
  other arithmetic: 4.75 us -> 0 us
    pallas_call x0 -> x1, Pallas kernels: none -> 34.9 us  [body(): pl.pallas_call(kernel, name='decode', out_shape=jax.ShapeDtypeStruct((use...]
    all_to_all x3 -> x0, starting transfers between devices: 30.8 us -> none  [the longest x1 23.7 us: sent_together(): lax.all_to_all(both, axis, split_axis=split_dim, concat_axis=concat_dim,...]
    all_to_all x3 -> x0, waiting for transfers between devices: 22.5 us -> none  [the longest x1 11 us: sent_together(): lax.all_to_all(both, axis, split_axis=split_dim, concat_axis=concat_dim,...]
    dot_general x5 -> x0, matrix products: 11.5 us -> none  [the longest x1 3.48 us: body(): jnp.einsum('uchd,ushd->uchs', query_heads, key_heads, preferred_element_t...]
    reduce_sum x7 -> x0, other arithmetic: 2.35 us -> none  [the longest x1 0.88 us: body(): local_squares = jnp.sum(jnp.square(attended), axis=(2, 3))]
    unnamed x6 -> x1, local copies, waits for them, and re-layouts: 0.01 us -> 1.28 us
    concatenate x1 -> x0, other arithmetic: 0.9 us -> none  [sent_together(): jnp.concatenate([a.reshape(*a.shape[:along], w) for a, w in zip(arrays, w...]
    lt x1 -> x0, other arithmetic: 0.74 us -> none  [body(): valid = position[None, None, None, :] < lengths[:, None, None, None]]
  transfers between devices with their start and end apart: 3 -> 0, of which waited for: 3 -> 0; matrix products, arithmetic and copies ran while one was open for 4% -> 0% of each run, Pallas kernels for 0% -> 0%
where the time goes in v1:
time: 36.3 us; the launch traced here: 36.2 us
  Pallas kernels  34.9 us (96%)
  local copies, waits for them, and re-layouts  1.28 us (4%)
    pallas_call x1, Pallas kernels, body(): pl.pallas_call(kernel, name='decode', out_shape=jax.ShapeDtypeStruct((use...  34.9 us
    unnamed x1, local copies, waits for them, and re-layouts  1.28 us

profile of v1, /device:TPU:513, one launch (start us, length us, event | category | flops | bytes accessed | tf_op | source)
XLA Modules:
  0.0 36.2 jit_solution(7209701040786903065)
XLA Ops:
  0.0 34.9 %decode.1 = bf16[1,16,128]{2,1,0:T(8,128)(2,1)} custom-call(bf16[16,16,128]{2,1,0:T(8,128)(2,1)} %query.1, bf16[16,16,128]{2,1,0:T(8,128)(2,1)} %new_key.1, bf16[16,16,128]{2,1,0:T(8,128)(2,1)} %new_value.1, bf16[16,1024,128]{2,1,0:T(8,128)(2,1)} %keys.1, bf16[16,1024,128]{2,1,0:T(8,128)(2,1)} %values.1, s32[16]{0:T(128)} %lengths.1, ...), custom_call_target="tpu_custom_call" | custom-call | tf_op jit(solution)/shard_map/decode/pallas_call | solution.py:284
  34.9 1.3 %copy.15 = bf16[1,16,128]{2,1,0:T(8,128)(2,1)} copy(bf16[1,16,128]{2,1,0:T(8,128)(2,1)} %decode.1) | data formatting | bytes 8192

commit v2 on v1

v2 whole, which is shorter than its diff:
```python
import math

import jax
import jax.numpy as jnp
from jax import lax
from jax.experimental import pallas as pl
from jax.experimental.pallas import tpu as pltpu
from jax.sharding import PartitionSpec as P

MESH = pl.DeviceIdType.MESH
LOG2E = math.log2(math.e)
LANES = 128
PAIR = 2
SPAN = 2


def far_first(count):
    return sorted(range(count), key=lambda d: (-min(d, count - d), d))


def lane_table(table):
    rows = jnp.broadcast_to(table, (8, table.shape[1]))
    rest = LANES - table.shape[1]
    if rest:
        rows = jnp.concatenate([rows, jnp.zeros((8, rest), rows.dtype)], axis=1)
    return rows


def kernel(
    query,
    new_key,
    new_value,
    keys,
    values,
    lengths,
    time_bucket,
    action,
    time_bias,
    action_bias,
    gate,
    norm_gain,
    w_out,
    out,
    q_buf,
    nk_buf,
    nv_buf,
    k_buf,
    v_buf,
    len_buf,
    tb_buf,
    ac_buf,
    tbias_buf,
    abias_buf,
    gate_buf,
    gain_buf,
    w_buf,
    bias_buf,
    score_buf,
    send1,
    recv1,
    send2,
    recv2,
    send3,
    recv3,
    in_sem,
    k_sem,
    v_sem,
    send_sem1,
    recv_sem1,
    send_sem2,
    recv_sem2,
    send_sem3,
    recv_sem3,
):
    n_seq = lax.axis_size("seq")
    n_head = lax.axis_size("head")
    n_chip = n_seq // PAIR
    me = lax.axis_index("seq")
    chip, core = lax.div(me, PAIR), lax.rem(me, PAIR)
    my_head = lax.axis_index("head")
    users, cands, width = query.shape
    block_len = keys.shape[1]
    pair_rows = PAIR * cands
    scale = LOG2E / math.sqrt(width)
    order = far_first(n_chip)
    f32, bf16 = jnp.float32, jnp.bfloat16

    def chip_at(e):
        return lax.rem(chip + e, n_chip)

    def head_at(e):
        return lax.rem(my_head + e, n_head)

    def pair_of(source, e):
        return source.at[pl.ds(chip_at(e) * PAIR, PAIR)]

    early = [
        (lengths, len_buf),
        (time_bias, tbias_buf),
        (action_bias, abias_buf),
        (time_bucket, tb_buf),
        (action, ac_buf),
        (query, q_buf),
    ]
    late = [
        (pair_of(new_key, 0), nk_buf),
        (pair_of(new_value, 0), nv_buf),
        (pair_of(gate, 0), gate_buf),
        (norm_gain, gain_buf),
        (w_out, w_buf),
    ]
    loads = [
        pltpu.make_async_copy(src, dst, in_sem.at[i]) for i, (src, dst) in enumerate(early + late)
    ]
    early, late = loads[: len(early)], loads[len(early) :]
    k_load = {e: pltpu.make_async_copy(pair_of(keys, e), k_buf.at[e], k_sem.at[e]) for e in order}
    v_load = {e: pltpu.make_async_copy(pair_of(values, e), v_buf.at[e], v_sem.at[e]) for e in order}
    spans = [order[i : i + SPAN] for i in range(0, n_chip, SPAN)]
    for load in early:
        load.start()
    for g, span in enumerate(spans):
        for e in span:
            k_load[e].start()
        for e in spans[g - 1] if g else ():
            v_load[e].start()
    for e in spans[-1]:
        v_load[e].start()
    for load in late:
        load.start()

    barrier = pltpu.get_barrier_semaphore()

    @pl.when(core == PAIR - 1)
    def _():
        for e in order:
            for c in range(PAIR):
                if e or c != PAIR - 1:
                    pl.semaphore_signal(
                        barrier,
                        inc=1,
                        device_id={"seq": chip_at(e) * PAIR + c},
                        device_id_type=MESH,
                    )
        for e in far_first(n_head)[:-1]:
            pl.semaphore_signal(barrier, inc=1, device_id={"head": head_at(e)}, device_id_type=MESH)

    for load in early:
        load.wait()
    row = lax.broadcasted_iota(jnp.int32, (users, LANES), 0)
    limit = jnp.zeros((users, LANES), jnp.int32)
    for u in range(users):
        limit = jnp.where(row == u, len_buf[u], limit)
    lane = lax.broadcasted_iota(jnp.int32, (8, LANES), 1)
    time_table, action_table = lane_table(tbias_buf[...]), lane_table(abias_buf[...])
    for r in range(0, users, 8):
        for c in range(0, block_len, LANES):
            bias = jnp.take_along_axis(
                time_table, tb_buf[r : r + 8, c : c + LANES], axis=1
            ) + jnp.take_along_axis(action_table, ac_buf[r : r + 8, c : c + LANES], axis=1)
            valid = me * block_len + c + lane < limit[r : r + 8]
            bias_buf[r : r + 8, c : c + LANES] = jnp.where(valid, bias * LOG2E, -1e30)

    diag = lax.broadcasted_iota(jnp.int32, (cands, LANES), 1) - lax.broadcasted_iota(
        jnp.int32, (cands, LANES), 0
    )

    def as_row(columns):
        spread = jnp.zeros((cands, LANES), f32)
        for k, column in columns.items():
            spread = jnp.where(diag == k * cands, column, spread)
        return jnp.sum(spread, axis=0, keepdims=True)

    def as_column(line, k):
        picked = jnp.where(diag == k * cands, line, 0.0)
        return jnp.sum(picked, axis=1, keepdims=True)

    def score(g):
        for i, e in enumerate(spans[g]):
            for c in range(PAIR):
                user = chip_at(e) * PAIR + c
                score_buf[g % 2, i, c] = (
                    lax.dot_general(
                        q_buf[user],
                        k_buf[e, c],
                        (((1,), (1,)), ((), ())),
                        preferred_element_type=f32,
                    )
                    * scale
                    + bias_buf[pl.ds(user, 1), :]
                )

    def soften(g):
        parts = {}
        for i, e in enumerate(spans[g]):
            for c in range(PAIR):
                scores = score_buf[g % 2, i, c]
                top = jnp.max(scores, axis=1, keepdims=True)
                weights = jnp.exp2(scores - top)
                parts[e, c] = (
                    top,
                    jnp.sum(weights, axis=1, keepdims=True),
                    weights.astype(bf16),
                )
        return parts

    def message(g, parts, place, e):
        columns = {}
        for c in range(PAIR):
            top, total, weights = parts[e, c]
            place[c * cands : (c + 1) * cands, :] = jnp.dot(
                weights, v_buf[e, c], preferred_element_type=f32
            )
            columns[2 * c], columns[2 * c + 1] = top, total
        place[pair_rows : pair_rows + 1, :] = as_row(columns)

    def to_owner(e):
        return pltpu.make_async_remote_copy(
            src_ref=send1.at[e],
            dst_ref=recv1.at[e, core],
            send_sem=send_sem1.at[e],
            recv_sem=recv_sem1.at[e, core],
            device_id={"seq": chip_at(e) * PAIR + PAIR - 1},
            device_id_type=MESH,
        )

    for e in spans[0]:
        k_load[e].wait()
    score(0)
    for g, span in enumerate(spans):
        for e in spans[g + 1] if g + 1 < len(spans) else ():
            k_load[e].wait()
        for e in span:
            v_load[e].wait()
        if g + 1 < len(spans):
            score(g + 1)
        parts = soften(g)
        for e in span:
            message(g, parts, send1.at[e], e)
        if g == 0:

            @pl.when(core == PAIR - 1)
            def _():
                pl.semaphore_wait(barrier, n_chip - 1 + n_head - 1)

            @pl.when(core != PAIR - 1)
            def _():
                pl.semaphore_wait(barrier, n_chip)

        for e in span:
            if e:
                to_owner(e).start()
    for load in late:
        load.wait()

    back = pltpu.make_async_remote_copy(
        src_ref=send3,
        dst_ref=recv3,
        send_sem=send_sem3,
        recv_sem=recv_sem3,
        device_id={"seq": chip * PAIR},
        device_id_type=MESH,
    )

    @pl.when(core != PAIR - 1)
    def _():
        to_owner(0).start()
        to_owner(0).wait_send()
        back.wait_recv()
        out[0] = recv3[...].astype(out.dtype)

    @pl.when(core == PAIR - 1)
    def _():
        own, own_value, gated = {}, {}, {}
        for c in range(PAIR):
            own_query = q_buf[chip * PAIR + c].astype(f32)
            own[2 * c] = (
                jnp.sum(own_query * nk_buf[c].astype(f32), axis=1, keepdims=True) * scale
            )
            own_value[c] = nv_buf[c].astype(f32)
            gates = gate_buf[c].astype(f32)
            gated[c] = gain_buf[...] * (gates / (1.0 + jnp.exp(-gates)))
        own = as_row(own)

        slots = [(e, c) for e in range(n_chip) for c in range(PAIR)]
        for e, c in slots:
            if e or c != PAIR - 1:
                pltpu.make_async_remote_copy(
                    src_ref=send1.at[e],
                    dst_ref=recv1.at[e, c],
                    send_sem=send_sem1.at[e],
                    recv_sem=recv_sem1.at[e, c],
                    device_id={"seq": chip * PAIR},
                    device_id_type=MESH,
                ).wait_recv()

        def slot(e, c):
            return recv1.at[e, c] if e or c != PAIR - 1 else send1.at[0]

        marks = jnp.zeros((len(slots), LANES), f32)
        place = lax.broadcasted_iota(jnp.int32, marks.shape, 0)
        for s, (e, c) in enumerate(slots):
            marks = jnp.where(place == s, slot(e, c)[pair_rows : pair_rows + 1, :], marks)
        overall = jnp.maximum(jnp.max(marks, axis=0, keepdims=True), own)
        factors = jnp.exp2(marks - overall)
        own_factor = jnp.exp2(own - overall)
        totals = pltpu.roll(marks, LANES - cands, 1)
        denom = own_factor + jnp.sum(factors * totals, axis=0, keepdims=True)
        hidden, squares = [], {}
        for c in range(PAIR):
            numer = as_column(own_factor, 2 * c) * own_value[c]
            for s, (e, k) in enumerate(slots):
                numer = numer + as_column(factors[s : s + 1], 2 * c) * slot(e, k)[
                    c * cands : (c + 1) * cands, :
                ]
            attended = numer / as_column(denom, 2 * c)
            squares[2 * c] = jnp.sum(attended * attended, axis=1, keepdims=True)
            hidden.append((attended * gated[c]).astype(bf16))
        hidden = jnp.concatenate(hidden, axis=0)
        squares = as_row(squares)
        for h in range(n_head):
            send2[h, 0:pair_rows, :] = jnp.dot(
                hidden, w_buf[:, h * width : (h + 1) * width], preferred_element_type=f32
            )
            send2[h, pair_rows : pair_rows + 1, :] = squares
        across = []
        for e in far_first(n_head)[:-1]:
            copy = pltpu.make_async_remote_copy(
                src_ref=send2.at[head_at(e)],
                dst_ref=recv2.at[e],
                send_sem=send_sem2.at[e],
                recv_sem=recv_sem2.at[e],
                device_id={"head": head_at(e)},
                device_id_type=MESH,
            )
            copy.start()
            across.append(copy)
        whole = send2[my_head]
        for copy in across:
            copy.wait_recv()
        for e in range(1, n_head):
            whole = whole + recv2[e]
        line = whole[pair_rows : pair_rows + 1]
        final = []
        for c in range(PAIR):
            square_sum = as_column(line, 2 * c)
            factor = 1.0 / jnp.sqrt(square_sum / (width * n_head) + 1e-06)
            final.append(whole[c * cands : (c + 1) * cands] * factor)
        send3[...] = final[0]
        back.start()
        out[0] = final[1].astype(out.dtype)
        for copy in across:
            copy.wait_send()
        back.wait_send()

    for e in order[:-1]:
        to_owner(e).wait_send()


def body(
    query,
    new_key,
    new_value,
    keys,
    values,
    lengths,
    time_bucket,
    action,
    time_bias,
    action_bias,
    gate,
    norm_gain,
    w_out,
):
    users, block_len, width = keys.shape
    cands = query.shape[1]
    n_seq, n_head = lax.axis_size("seq"), lax.axis_size("head")
    assert users == n_seq and width == LANES and w_out.shape[1] == n_head * width
    assert n_seq % (PAIR * SPAN) == 0 and 4 * cands <= LANES
    n_chip = n_seq // PAIR
    tile = PAIR * cands + 1
    bf16, f32, i32 = jnp.bfloat16, jnp.float32, jnp.int32
    vmem, dma = pltpu.VMEM, pltpu.SemaphoreType.DMA
    buckets, actions = time_bias.shape[0], action_bias.shape[0]
    return pl.pallas_call(
        kernel,
        name="decode",
        out_shape=jax.ShapeDtypeStruct((users // n_seq, cands, width), bf16),
        in_specs=[pl.BlockSpec(memory_space=pl.ANY)] * 13,
        out_specs=pl.BlockSpec(memory_space=vmem),
        scratch_shapes=[
            vmem((users, cands, width), bf16),
            vmem((PAIR, cands, width), bf16),
            vmem((PAIR, cands, width), bf16),
            vmem((n_chip, PAIR, block_len, width), bf16),
            vmem((n_chip, PAIR, block_len, width), bf16),
            pltpu.SMEM((users,), i32),
            vmem((users, block_len), i32),
            vmem((users, block_len), i32),
            vmem((1, buckets), f32),
            vmem((1, actions), f32),
            vmem((PAIR, cands, width), bf16),
            vmem((1, width), f32),
            vmem((width, n_head * width), bf16),
            vmem((users, block_len), f32),
            vmem((2, SPAN, PAIR, cands, block_len), f32),
            vmem((n_chip, tile, width), f32),
            vmem((n_chip, PAIR, tile, width), f32),
            vmem((n_head, tile, width), f32),
            vmem((n_head, tile, width), f32),
            vmem((cands, width), f32),
            vmem((cands, width), f32),
            dma((11,)),
            dma((n_chip,)),
            dma((n_chip,)),
            dma((n_chip,)),
            dma((n_chip, PAIR)),
            dma((n_head,)),
            dma((n_head,)),
            dma,
            dma,
        ],
        compiler_params=pltpu.CompilerParams(collective_id=0, has_side_effects=True),
    )(
        query,
        new_key,
        new_value,
        keys,
        values,
        lengths,
        time_bucket,
        action,
        time_bias.reshape(1, buckets),
        action_bias.reshape(1, actions),
        gate,
        norm_gain.reshape(1, width),
        w_out,
    )


def solution(mesh):
    placed = (
        P("groups", None, "head"),
        P("groups", None, "head"),
        P("groups", None, "head"),
        P("groups", "seq", "head"),
        P("groups", "seq", "head"),
        P("groups"),
        P("groups", "seq"),
        P("groups", "seq"),
        P(None, "head"),
        P(None, "head"),
        P("groups", None, "head"),
        P("head"),
        P("head", None),
    )
    return jax.shard_map(
        body,
        mesh=mesh,
        in_specs=placed,
        out_specs=P(("groups", "seq"), None, "head"),
        check_vma=False,
    )
```

time: 36.3 us -> 30.2 us (0.83)
  the two profiles are of different devices: /device:TPU:513 before, /device:TPU:515 now
where the time goes in v2:
time: 30.2 us; the launch traced here: 30.1 us
  Pallas kernels  28.8 us (95%)
  local copies, waits for them, and re-layouts  1.28 us (4%)
    pallas_call x1, Pallas kernels, body(): pl.pallas_call(kernel, name='decode', out_shape=jax.ShapeDtypeStruct((use...  28.8 us
    unnamed x1, local copies, waits for them, and re-layouts  1.28 us

profile of v2, /device:TPU:515, one launch (start us, length us, event | category | flops | bytes accessed | tf_op | source)
XLA Modules:
  0.0 30.1 jit_solution(5497336256520406539)
XLA Ops:
  0.0 28.8 %decode.1 = bf16[1,16,128]{2,1,0:T(8,128)(2,1)} custom-call(bf16[16,16,128]{2,1,0:T(8,128)(2,1)} %query.1, bf16[16,16,128]{2,1,0:T(8,128)(2,1)} %new_key.1, bf16[16,16,128]{2,1,0:T(8,128)(2,1)} %new_value.1, bf16[16,1024,128]{2,1,0:T(8,128)(2,1)} %keys.1, bf16[16,1024,128]{2,1,0:T(8,128)(2,1)} %values.1, s32[16]{0:T(128)} %lengths.1, ...), custom_call_target="tpu_custom_call" | custom-call | tf_op jit(solution)/shard_map/decode/pallas_call | solution.py:384
  28.8 1.3 %copy.15 = bf16[1,16,128]{2,1,0:T(8,128)(2,1)} copy(bf16[1,16,128]{2,1,0:T(8,128)(2,1)} %decode.1) | data formatting | bytes 8192

commit v3 on v2

--- a/solution.py
+++ b/solution.py
@@ -82,7 +82,7 @@
     block_len = keys.shape[1]
     pair_rows = PAIR * cands
     scale = LOG2E / math.sqrt(width)
-    order = far_first(n_chip)
+    order = [0, 1] + [e for e in far_first(n_chip) if e > 1]
     f32, bf16 = jnp.float32, jnp.bfloat16
 
     def chip_at(e):
@@ -95,12 +95,12 @@
         return source.at[pl.ds(chip_at(e) * PAIR, PAIR)]
 
     early = [
+        (query, q_buf),
         (lengths, len_buf),
         (time_bias, tbias_buf),
         (action_bias, abias_buf),
         (time_bucket, tb_buf),
         (action, ac_buf),
-        (query, q_buf),
     ]
     late = [
         (pair_of(new_key, 0), nk_buf),
@@ -116,10 +116,13 @@
     k_load = {e: pltpu.make_async_copy(pair_of(keys, e), k_buf.at[e], k_sem.at[e]) for e in order}
     v_load = {e: pltpu.make_async_copy(pair_of(values, e), v_buf.at[e], v_sem.at[e]) for e in order}
     spans = [order[i : i + SPAN] for i in range(0, n_chip, SPAN)]
-    for load in early:
+    early[0].start()
+    for e in spans[0]:
+        k_load[e].start()
+    for load in early[1:]:
         load.start()
     for g, span in enumerate(spans):
-        for e in span:
+        for e in span if g else ():
             k_load[e].start()
         for e in spans[g - 1] if g else ():
             v_load[e].start()
@@ -132,7 +135,7 @@
 
     @pl.when(core == PAIR - 1)
     def _():
-        for e in order:
+        for e in far_first(n_chip):
             for c in range(PAIR):
                 if e or c != PAIR - 1:
                     pl.semaphore_signal(
@@ -144,7 +147,67 @@
         for e in far_first(n_head)[:-1]:
             pl.semaphore_signal(barrier, inc=1, device_id={"head": head_at(e)}, device_id_type=MESH)
 
-    for load in early:
+    diag = lax.broadcasted_iota(jnp.int32, (cands, LANES), 1) - lax.broadcasted_iota(
+        jnp.int32, (cands, LANES), 0
+    )
+
+    def as_row(columns):
+        spread = jnp.zeros((cands, LANES), f32)
+        for k, column in columns.items():
+            spread = jnp.where(diag == k * cands, column, spread)
+        return jnp.sum(spread, axis=0, keepdims=True)
+
+    def as_column(line, k):
+        picked = jnp.where(diag == k * cands, line, 0.0)
+        return jnp.sum(picked, axis=1, keepdims=True)
+
+    def score(g):
+        for e in spans[g]:
+            for c in range(PAIR):
+                score_buf[e, c] = lax.dot_general(
+                    q_buf[chip_at(e) * PAIR + c],
+                    k_buf[e, c],
+                    (((1,), (1,)), ((), ())),
+                    preferred_element_type=f32,
+                )
+
+    def soften(g):
+        parts = {}
+        for e in spans[g]:
+            columns = {}
+            for c in range(PAIR):
+                user = chip_at(e) * PAIR + c
+                scores = score_buf[e, c] * scale + bias_buf[pl.ds(user, 1), :]
+                top = jnp.max(scores, axis=1, keepdims=True)
+                weights = jnp.exp2(scores - top)
+                parts[e, c] = weights.astype(bf16)
+                columns[2 * c] = top
+                columns[2 * c + 1] = jnp.sum(weights, axis=1, keepdims=True)
+            send1[e, pair_rows : pair_rows + 1, :] = as_row(columns)
+        return parts
+
+    def weigh(parts, e):
+        for c in range(PAIR):
+            send1[e, c * cands : (c + 1) * cands, :] = jnp.dot(
+                parts[e, c], v_buf[e, c], preferred_element_type=f32
+            )
+
+    def to_owner(e):
+        return pltpu.make_async_remote_copy(
+            src_ref=send1.at[e],
+            dst_ref=recv1.at[e, core],
+            send_sem=send_sem1.at[e],
+            recv_sem=recv_sem1.at[e, core],
+            device_id={"seq": chip_at(e) * PAIR + PAIR - 1},
+            device_id_type=MESH,
+        )
+
+    early[0].wait()
+    for e in spans[0]:
+        k_load[e].wait()
+    score(0)
+
+    for load in early[1:]:
         load.wait()
     row = lax.broadcasted_iota(jnp.int32, (users, LANES), 0)
     limit = jnp.zeros((users, LANES), jnp.int32)
@@ -160,95 +223,34 @@
             valid = me * block_len + c + lane < limit[r : r + 8]
             bias_buf[r : r + 8, c : c + LANES] = jnp.where(valid, bias * LOG2E, -1e30)
 
-    diag = lax.broadcasted_iota(jnp.int32, (cands, LANES), 1) - lax.broadcasted_iota(
-        jnp.int32, (cands, LANES), 0
-    )
-
-    def as_row(columns):
-        spread = jnp.zeros((cands, LANES), f32)
-        for k, column in columns.items():
-            spread = jnp.where(diag == k * cands, column, spread)
-        return jnp.sum(spread, axis=0, keepdims=True)
-
-    def as_column(line, k):
-        picked = jnp.where(diag == k * cands, line, 0.0)
-        return jnp.sum(picked, axis=1, keepdims=True)
-
-    def score(g):
-        for i, e in enumerate(spans[g]):
-            for c in range(PAIR):
-                user = chip_at(e) * PAIR + c
-                score_buf[g % 2, i, c] = (
-                    lax.dot_general(
-                        q_buf[user],
-                        k_buf[e, c],
-                        (((1,), (1,)), ((), ())),
-                        preferred_element_type=f32,
-                    )
-                    * scale
-                    + bias_buf[pl.ds(user, 1), :]
-                )
-
-    def soften(g):
-        parts = {}
-        for i, e in enumerate(spans[g]):
-            for c in range(PAIR):
-                scores = score_buf[g % 2, i, c]
-                top = jnp.max(scores, axis=1, keepdims=True)
-                weights = jnp.exp2(scores - top)
-                parts[e, c] = (
-                    top,
-                    jnp.sum(weights, axis=1, keepdims=True),
-                    weights.astype(bf16),
-                )
-        return parts
-
-    def message(g, parts, place, e):
-        columns = {}
-        for c in range(PAIR):
-            top, total, weights = parts[e, c]
-            place[c * cands : (c + 1) * cands, :] = jnp.dot(
-                weights, v_buf[e, c], preferred_element_type=f32
-            )
-            columns[2 * c], columns[2 * c + 1] = top, total
-        place[pair_rows : pair_rows + 1, :] = as_row(columns)
-
-    def to_owner(e):
-        return pltpu.make_async_remote_copy(
-            src_ref=send1.at[e],
-            dst_ref=recv1.at[e, core],
-            send_sem=send_sem1.at[e],
-            recv_sem=recv_sem1.at[e, core],
-            device_id={"seq": chip_at(e) * PAIR + PAIR - 1},
-            device_id_type=MESH,
-        )
-
-    for e in spans[0]:
-        k_load[e].wait()
-    score(0)
     for g, span in enumerate(spans):
-        for e in spans[g + 1] if g + 1 < len(spans) else ():
-            k_load[e].wait()
+        if g + 1 < len(spans):
+            for e in spans[g + 1]:
+                k_load[e].wait()
+            for e in span:
+                v_load[e].wait()
+            score(g + 1)
+            parts = soften(g)
+        else:
+            parts = soften(g)
+            for e in span:
+                v_load[e].wait()
         for e in span:
-            v_load[e].wait()
-        if g + 1 < len(spans):
-            score(g + 1)
-        parts = soften(g)
-        for e in span:
-            message(g, parts, send1.at[e], e)
-        if g == 0:
-
-            @pl.when(core == PAIR - 1)
-            def _():
-                pl.semaphore_wait(barrier, n_chip - 1 + n_head - 1)
-
-            @pl.when(core != PAIR - 1)
-            def _():
+            weigh(parts, e)
+
+        @pl.when(core != PAIR - 1)
+        def _():
+            if g == 0:
                 pl.semaphore_wait(barrier, n_chip)
-
-        for e in span:
-            if e:
+            for e in span:
                 to_owner(e).start()
+
+    @pl.when(core == PAIR - 1)
+    def _():
+        pl.semaphore_wait(barrier, n_chip - 1 + n_head - 1)
+        for e in far_first(n_chip)[:-1]:
+            to_owner(e).start()
+
     for load in late:
         load.wait()
 
@@ -263,10 +265,9 @@
 
     @pl.when(core != PAIR - 1)
     def _():
-        to_owner(0).start()
-        to_owner(0).wait_send()
         back.wait_recv()
         out[0] = recv3[...].astype(out.dtype)
+        to_owner(0).wait_send()
 
     @pl.when(core == PAIR - 1)
     def _():
@@ -352,7 +353,7 @@
             copy.wait_send()
         back.wait_send()
 
-    for e in order[:-1]:
+    for e in order[1:]:
         to_owner(e).wait_send()
 
 
@@ -384,7 +385,7 @@
     return pl.pallas_call(
         kernel,
         name="decode",
-        out_shape=jax.ShapeDtypeStruct((users // n_seq, cands, width), bf16),
+        out_shape=pltpu.VMEM((users // n_seq, cands, width), bf16),
         in_specs=[pl.BlockSpec(memory_space=pl.ANY)] * 13,
         out_specs=pl.BlockSpec(memory_space=vmem),
         scratch_shapes=[
@@ -402,7 +403,7 @@
             vmem((1, width), f32),
             vmem((width, n_head * width), bf16),
             vmem((users, block_len), f32),
-            vmem((2, SPAN, PAIR, cands, block_len), f32),
+            vmem((n_chip, PAIR, cands, block_len), f32),
             vmem((n_chip, tile, width), f32),
             vmem((n_chip, PAIR, tile, width), f32),
             vmem((n_head, tile, width), f32),

time: 30.2 us -> 29.5 us (0.977)
  the two profiles are of different devices: /device:TPU:515 before, /device:TPU:513 now
where the time goes in v3:
time: 29.5 us; the launch traced here: 29.4 us
  Pallas kernels  28.8 us (98%)
  local copies, waits for them, and re-layouts  0.6 us (2%)
    pallas_call x1, Pallas kernels, body(): pl.pallas_call(kernel, name='decode', out_shape=pltpu.VMEM((users // n_se...  28.8 us
    unnamed x1, local copies, waits for them, and re-layouts  0.6 us

profile of v3, /device:TPU:513, one launch (start us, length us, event | category | flops | bytes accessed | tf_op | source)
XLA Modules:
  0.0 29.4 jit_solution(16944114721574622014)
XLA Ops:
  0.0 28.8 %decode.1 = bf16[1,16,128]{2,1,0:T(8,128)(2,1)S(1)} custom-call(bf16[16,16,128]{2,1,0:T(8,128)(2,1)} %query.1, bf16[16,16,128]{2,1,0:T(8,128)(2,1)} %new_key.1, bf16[16,16,128]{2,1,0:T(8,128)(2,1)} %new_value.1, bf16[16,1024,128]{2,1,0:T(8,128)(2,1)} %keys.1, bf16[16,1024,128]{2,1,0:T(8,128)(2,1)} %values.1, s32[16]{0:T(128)} %lengths.1, ...), custom_call_target="tpu_custom_call" | custom-call | tf_op jit(solution)/shard_map/decode/pallas_call | solution.py:385
  28.8 0.6 %copy.15 = bf16[1,16,128]{2,1,0:T(8,128)(2,1)} copy(bf16[1,16,128]{2,1,0:T(8,128)(2,1)S(1)} %decode.1) | data formatting | bytes 8192

commit v4 on v3

--- a/solution.py
+++ b/solution.py
@@ -60,8 +60,6 @@
     recv1,
     send2,
     recv2,
-    send3,
-    recv3,
     in_sem,
     k_sem,
     v_sem,
@@ -69,8 +67,7 @@
     recv_sem1,
     send_sem2,
     recv_sem2,
-    send_sem3,
-    recv_sem3,
+    ring_sem,
 ):
     n_seq = lax.axis_size("seq")
     n_head = lax.axis_size("head")
@@ -82,7 +79,8 @@
     block_len = keys.shape[1]
     pair_rows = PAIR * cands
     scale = LOG2E / math.sqrt(width)
-    order = [0, 1] + [e for e in far_first(n_chip) if e > 1]
+    far = far_first(n_chip)[:-1]
+    order = [0, far[0], 1] + [e for e in far[1:] if e != 1]
     f32, bf16 = jnp.float32, jnp.bfloat16
 
     def chip_at(e):
@@ -113,21 +111,25 @@
         pltpu.make_async_copy(src, dst, in_sem.at[i]) for i, (src, dst) in enumerate(early + late)
     ]
     early, late = loads[: len(early)], loads[len(early) :]
-    k_load = {e: pltpu.make_async_copy(pair_of(keys, e), k_buf.at[e], k_sem.at[e]) for e in order}
-    v_load = {e: pltpu.make_async_copy(pair_of(values, e), v_buf.at[e], v_sem.at[e]) for e in order}
     spans = [order[i : i + SPAN] for i in range(0, n_chip, SPAN)]
+
+    def start_span(source, buf, sem, g):
+        for i, e in enumerate(spans[g]):
+            pltpu.make_async_copy(
+                pair_of(source, e), buf.at[g, pl.ds(i * PAIR, PAIR)], sem.at[g]
+            ).start()
+
+    def wait_span(source, buf, sem, g):
+        pltpu.make_async_copy(source.at[pl.ds(0, SPAN * PAIR)], buf.at[g], sem.at[g]).wait()
+
     early[0].start()
-    for e in spans[0]:
-        k_load[e].start()
+    start_span(keys, k_buf, k_sem, 0)
     for load in early[1:]:
         load.start()
-    for g, span in enumerate(spans):
-        for e in span if g else ():
-            k_load[e].start()
-        for e in spans[g - 1] if g else ():
-            v_load[e].start()
-    for e in spans[-1]:
-        v_load[e].start()
+    for g in range(1, len(spans)):
+        start_span(keys, k_buf, k_sem, g)
+        start_span(values, v_buf, v_sem, g - 1)
+    start_span(values, v_buf, v_sem, len(spans) - 1)
     for load in late:
         load.start()
 
@@ -135,17 +137,18 @@
 
     @pl.when(core == PAIR - 1)
     def _():
-        for e in far_first(n_chip):
-            for c in range(PAIR):
-                if e or c != PAIR - 1:
-                    pl.semaphore_signal(
-                        barrier,
-                        inc=1,
-                        device_id={"seq": chip_at(e) * PAIR + c},
-                        device_id_type=MESH,
-                    )
-        for e in far_first(n_head)[:-1]:
-            pl.semaphore_signal(barrier, inc=1, device_id={"head": head_at(e)}, device_id_type=MESH)
+        for e in far + [0]:
+            pl.semaphore_signal(
+                barrier, inc=1, device_id={"seq": chip_at(e) * PAIR}, device_id_type=MESH
+            )
+
+    for e in far_first(n_head)[:-1]:
+        pl.semaphore_signal(
+            barrier,
+            inc=1,
+            device_id={"seq": chip * PAIR + PAIR - 1, "head": head_at(e)},
+            device_id_type=MESH,
+        )
 
     diag = lax.broadcasted_iota(jnp.int32, (cands, LANES), 1) - lax.broadcasted_iota(
         jnp.int32, (cands, LANES), 0
@@ -162,11 +165,11 @@
         return jnp.sum(picked, axis=1, keepdims=True)
 
     def score(g):
-        for e in spans[g]:
+        for i, e in enumerate(spans[g]):
             for c in range(PAIR):
                 score_buf[e, c] = lax.dot_general(
                     q_buf[chip_at(e) * PAIR + c],
-                    k_buf[e, c],
+                    k_buf[g, i * PAIR + c],
                     (((1,), (1,)), ((), ())),
                     preferred_element_type=f32,
                 )
@@ -186,25 +189,25 @@
             send1[e, pair_rows : pair_rows + 1, :] = as_row(columns)
         return parts
 
-    def weigh(parts, e):
-        for c in range(PAIR):
-            send1[e, c * cands : (c + 1) * cands, :] = jnp.dot(
-                parts[e, c], v_buf[e, c], preferred_element_type=f32
-            )
+    def weigh(g, parts):
+        for i, e in enumerate(spans[g]):
+            for c in range(PAIR):
+                send1[e, c * cands : (c + 1) * cands, :] = jnp.dot(
+                    parts[e, c], v_buf[g, i * PAIR + c], preferred_element_type=f32
+                )
 
     def to_owner(e):
         return pltpu.make_async_remote_copy(
             src_ref=send1.at[e],
-            dst_ref=recv1.at[e, core],
-            send_sem=send_sem1.at[e],
-            recv_sem=recv_sem1.at[e, core],
+            dst_ref=recv1.at[e * PAIR - 1 + core if e else 0],
+            send_sem=send_sem1,
+            recv_sem=recv_sem1,
             device_id={"seq": chip_at(e) * PAIR + PAIR - 1},
             device_id_type=MESH,
         )
 
     early[0].wait()
-    for e in spans[0]:
-        k_load[e].wait()
+    wait_span(keys, k_buf, k_sem, 0)
     score(0)
 
     for load in early[1:]:
@@ -223,51 +226,85 @@
             valid = me * block_len + c + lane < limit[r : r + 8]
             bias_buf[r : r + 8, c : c + LANES] = jnp.where(valid, bias * LOG2E, -1e30)
 
+    ready = len(spans) - 2
     for g, span in enumerate(spans):
         if g + 1 < len(spans):
-            for e in spans[g + 1]:
-                k_load[e].wait()
-            for e in span:
-                v_load[e].wait()
+            wait_span(keys, k_buf, k_sem, g + 1)
+            wait_span(values, v_buf, v_sem, g)
             score(g + 1)
             parts = soften(g)
         else:
             parts = soften(g)
-            for e in span:
-                v_load[e].wait()
-        for e in span:
-            weigh(parts, e)
+            wait_span(values, v_buf, v_sem, g)
+        weigh(g, parts)
 
         @pl.when(core != PAIR - 1)
         def _():
             if g == 0:
                 pl.semaphore_wait(barrier, n_chip)
+                pl.semaphore_signal(
+                    ring_sem, inc=1, device_id={"seq": me + 1}, device_id_type=MESH
+                )
             for e in span:
                 to_owner(e).start()
 
-    @pl.when(core == PAIR - 1)
-    def _():
-        pl.semaphore_wait(barrier, n_chip - 1 + n_head - 1)
-        for e in far_first(n_chip)[:-1]:
-            to_owner(e).start()
+        if g >= ready:
+
+            @pl.when(core == PAIR - 1)
+            def _():
+                if g == ready:
+                    pl.semaphore_wait(ring_sem, 1)
+                done = order[: (ready + 1) * SPAN] if g == ready else span
+                for e in far:
+                    if e in done:
+                        to_owner(e).start()
 
     for load in late:
         load.wait()
 
-    back = pltpu.make_async_remote_copy(
-        src_ref=send3,
-        dst_ref=recv3,
-        send_sem=send_sem3,
-        recv_sem=recv_sem3,
-        device_id={"seq": chip * PAIR},
-        device_id_type=MESH,
-    )
+    def across(e, c):
+        return pltpu.make_async_remote_copy(
+            src_ref=send2.at[head_at(e) * PAIR + c],
+            dst_ref=recv2.at[e],
+            send_sem=send_sem2,
+            recv_sem=recv_sem2,
+            device_id={"seq": chip * PAIR + c, "head": head_at(e)},
+            device_id_type=MESH,
+        )
+
+    def arrived(buf, sem):
+        pltpu.make_async_remote_copy(
+            src_ref=buf,
+            dst_ref=buf,
+            send_sem=send_sem2,
+            recv_sem=sem,
+            device_id={"seq": chip * PAIR + PAIR - 1 - core},
+            device_id_type=MESH,
+        ).wait_recv()
+
+    def gone(buf, sem):
+        pltpu.make_async_remote_copy(
+            src_ref=buf,
+            dst_ref=buf,
+            send_sem=sem,
+            recv_sem=recv_sem2,
+            device_id={"seq": chip * PAIR + PAIR - 1 - core},
+            device_id_type=MESH,
+        ).wait_send()
+
+    def finish():
+        whole = recv2[0]
+        for e in range(1, n_head):
+            whole = whole + recv2[e]
+        square_sum = as_column(whole[cands : cands + 1], 0)
+        factor = 1.0 / jnp.sqrt(square_sum / (width * n_head) + 1e-06)
+        out[0] = (whole[:cands] * factor).astype(out.dtype)
 
     @pl.when(core != PAIR - 1)
     def _():
-        back.wait_recv()
-        out[0] = recv3[...].astype(out.dtype)
-        to_owner(0).wait_send()
+        arrived(recv2, recv_sem2)
+        finish()
+        gone(send1, send_sem1)
 
     @pl.when(core == PAIR - 1)
     def _():
@@ -281,26 +318,13 @@
             gates = gate_buf[c].astype(f32)
             gated[c] = gain_buf[...] * (gates / (1.0 + jnp.exp(-gates)))
         own = as_row(own)
-
-        slots = [(e, c) for e in range(n_chip) for c in range(PAIR)]
-        for e, c in slots:
-            if e or c != PAIR - 1:
-                pltpu.make_async_remote_copy(
-                    src_ref=send1.at[e],
-                    dst_ref=recv1.at[e, c],
-                    send_sem=send_sem1.at[e],
-                    recv_sem=recv_sem1.at[e, c],
-                    device_id={"seq": chip * PAIR},
-                    device_id_type=MESH,
-                ).wait_recv()
-
-        def slot(e, c):
-            return recv1.at[e, c] if e or c != PAIR - 1 else send1.at[0]
-
-        marks = jnp.zeros((len(slots), LANES), f32)
+        arrived(recv1, recv_sem1)
+
+        slots = [recv1.at[i] for i in range(n_seq - 1)] + [send1.at[0]]
+        marks = jnp.zeros((n_seq, LANES), f32)
         place = lax.broadcasted_iota(jnp.int32, marks.shape, 0)
-        for s, (e, c) in enumerate(slots):
-            marks = jnp.where(place == s, slot(e, c)[pair_rows : pair_rows + 1, :], marks)
+        for i, slot in enumerate(slots):
+            marks = jnp.where(place == i, slot[pair_rows : pair_rows + 1, :], marks)
         overall = jnp.maximum(jnp.max(marks, axis=0, keepdims=True), own)
         factors = jnp.exp2(marks - overall)
         own_factor = jnp.exp2(own - overall)
@@ -309,52 +333,31 @@
         hidden, squares = [], {}
         for c in range(PAIR):
             numer = as_column(own_factor, 2 * c) * own_value[c]
-            for s, (e, k) in enumerate(slots):
-                numer = numer + as_column(factors[s : s + 1], 2 * c) * slot(e, k)[
+            for i, slot in enumerate(slots):
+                numer = numer + as_column(factors[i : i + 1], 2 * c) * slot[
                     c * cands : (c + 1) * cands, :
                 ]
             attended = numer / as_column(denom, 2 * c)
-            squares[2 * c] = jnp.sum(attended * attended, axis=1, keepdims=True)
+            squares[c] = as_row({0: jnp.sum(attended * attended, axis=1, keepdims=True)})
             hidden.append((attended * gated[c]).astype(bf16))
         hidden = jnp.concatenate(hidden, axis=0)
-        squares = as_row(squares)
         for h in range(n_head):
-            send2[h, 0:pair_rows, :] = jnp.dot(
+            part = jnp.dot(
                 hidden, w_buf[:, h * width : (h + 1) * width], preferred_element_type=f32
             )
-            send2[h, pair_rows : pair_rows + 1, :] = squares
-        across = []
+            for c in range(PAIR):
+                send2[h * PAIR + c, 0:cands, :] = part[c * cands : (c + 1) * cands]
+                send2[h * PAIR + c, cands : cands + 1, :] = squares[c]
+        pl.semaphore_wait(barrier, PAIR * (n_head - 1))
         for e in far_first(n_head)[:-1]:
-            copy = pltpu.make_async_remote_copy(
-                src_ref=send2.at[head_at(e)],
-                dst_ref=recv2.at[e],
-                send_sem=send_sem2.at[e],
-                recv_sem=recv_sem2.at[e],
-                device_id={"head": head_at(e)},
-                device_id_type=MESH,
-            )
-            copy.start()
-            across.append(copy)
-        whole = send2[my_head]
-        for copy in across:
-            copy.wait_recv()
-        for e in range(1, n_head):
-            whole = whole + recv2[e]
-        line = whole[pair_rows : pair_rows + 1]
-        final = []
-        for c in range(PAIR):
-            square_sum = as_column(line, 2 * c)
-            factor = 1.0 / jnp.sqrt(square_sum / (width * n_head) + 1e-06)
-            final.append(whole[c * cands : (c + 1) * cands] * factor)
-        send3[...] = final[0]
-        back.start()
-        out[0] = final[1].astype(out.dtype)
-        for copy in across:
-            copy.wait_send()
-        back.wait_send()
-
-    for e in order[1:]:
-        to_owner(e).wait_send()
+            for c in range(PAIR):
+                across(e, c).start()
+        across(0, 0).start()
+        recv2[0] = send2[my_head * PAIR + PAIR - 1]
+        arrived(recv2.at[pl.ds(1, n_head - 1)], recv_sem2)
+        finish()
+        gone(send1.at[pl.ds(1, n_chip - 1)], send_sem1)
+        gone(send2.at[pl.ds(0, n_head * PAIR - 1)], send_sem2)
 
 
 def body(
@@ -392,8 +395,8 @@
             vmem((users, cands, width), bf16),
             vmem((PAIR, cands, width), bf16),
             vmem((PAIR, cands, width), bf16),
-            vmem((n_chip, PAIR, block_len, width), bf16),
-            vmem((n_chip, PAIR, block_len, width), bf16),
+            vmem((n_chip // SPAN, SPAN * PAIR, block_len, width), bf16),
+            vmem((n_chip // SPAN, SPAN * PAIR, block_len, width), bf16),
             pltpu.SMEM((users,), i32),
             vmem((users, block_len), i32),
             vmem((users, block_len), i32),
@@ -405,20 +408,17 @@
             vmem((users, block_len), f32),
             vmem((n_chip, PAIR, cands, block_len), f32),
             vmem((n_chip, tile, width), f32),
-            vmem((n_chip, PAIR, tile, width), f32),
-            vmem((n_head, tile, width), f32),
-            vmem((n_head, tile, width), f32),
-            vmem((cands, width), f32),
-            vmem((cands, width), f32),
+            vmem((n_seq - 1, tile, width), f32),
+            vmem((n_head * PAIR, cands + 1, width), f32),
+            vmem((n_head, cands + 1, width), f32),
             dma((11,)),
-            dma((n_chip,)),
-            dma((n_chip,)),
-            dma((n_chip,)),
-            dma((n_chip, PAIR)),
-            dma((n_head,)),
-            dma((n_head,)),
+            dma((n_chip // SPAN,)),
+            dma((n_chip // SPAN,)),
             dma,
             dma,
+            dma,
+            dma,
+            pltpu.SemaphoreType.REGULAR,
         ],
         compiler_params=pltpu.CompilerParams(collective_id=0, has_side_effects=True),
     )(

time: 29.5 us -> 28.2 us (0.956)
  Pallas kernels: 28.8 us -> 27.5 us
    pallas_call x1, Pallas kernels: 28.8 us -> 27.5 us  [body(): pl.pallas_call(kernel, name='decode', out_shape=pltpu.VMEM((users // n_se...]
where the time goes in v4:
time: 28.2 us; the launch traced here: 28.1 us
  Pallas kernels  27.5 us (98%)
  local copies, waits for them, and re-layouts  0.6 us (2%)
    pallas_call x1, Pallas kernels, body(): pl.pallas_call(kernel, name='decode', out_shape=pltpu.VMEM((users // n_se...  27.5 us
    unnamed x1, local copies, waits for them, and re-layouts  0.6 us

profile of v4, /device:TPU:513, one launch (start us, length us, event | category | flops | bytes accessed | tf_op | source)
XLA Modules:
  0.0 28.1 jit_solution(10925628697494079529)
XLA Ops:
  0.0 27.5 %decode.1 = bf16[1,16,128]{2,1,0:T(8,128)(2,1)S(1)} custom-call(bf16[16,16,128]{2,1,0:T(8,128)(2,1)} %query.1, bf16[16,16,128]{2,1,0:T(8,128)(2,1)} %new_key.1, bf16[16,16,128]{2,1,0:T(8,128)(2,1)} %new_value.1, bf16[16,1024,128]{2,1,0:T(8,128)(2,1)} %keys.1, bf16[16,1024,128]{2,1,0:T(8,128)(2,1)} %values.1, s32[16]{0:T(128)} %lengths.1, ...), custom_call_target="tpu_custom_call" | custom-call | tf_op jit(solution)/shard_map/decode/pallas_call | solution.py:388
  27.5 0.6 %copy.15 = bf16[1,16,128]{2,1,0:T(8,128)(2,1)} copy(bf16[1,16,128]{2,1,0:T(8,128)(2,1)S(1)} %decode.1) | data formatting | bytes 8192

commit v5 on v4

--- a/solution.py
+++ b/solution.py
@@ -67,7 +67,7 @@
     recv_sem1,
     send_sem2,
     recv_sem2,
-    ring_sem,
+    told,
 ):
     n_seq = lax.axis_size("seq")
     n_head = lax.axis_size("head")
@@ -137,17 +137,26 @@
 
     @pl.when(core == PAIR - 1)
     def _():
-        for e in far + [0]:
+        for e in far:
             pl.semaphore_signal(
-                barrier, inc=1, device_id={"seq": chip_at(e) * PAIR}, device_id_type=MESH
+                barrier,
+                inc=1,
+                device_id={"seq": chip_at(e) * PAIR + PAIR - 1},
+                device_id_type=MESH,
             )
 
+    @pl.when(core != PAIR - 1)
+    def _():
+        pl.semaphore_signal(
+            barrier, inc=1, device_id={"seq": chip * PAIR + PAIR - 1}, device_id_type=MESH
+        )
+
     for e in far_first(n_head)[:-1]:
+        pl.semaphore_signal(barrier, inc=1, device_id={"head": head_at(e)}, device_id_type=MESH)
+
+    def tell_partner():
         pl.semaphore_signal(
-            barrier,
-            inc=1,
-            device_id={"seq": chip * PAIR + PAIR - 1, "head": head_at(e)},
-            device_id_type=MESH,
+            told, inc=1, device_id={"seq": chip * PAIR + PAIR - 1 - core}, device_id_type=MESH
         )
 
     diag = lax.broadcasted_iota(jnp.int32, (cands, LANES), 1) - lax.broadcasted_iota(
@@ -226,7 +235,6 @@
             valid = me * block_len + c + lane < limit[r : r + 8]
             bias_buf[r : r + 8, c : c + LANES] = jnp.where(valid, bias * LOG2E, -1e30)
 
-    ready = len(spans) - 2
     for g, span in enumerate(spans):
         if g + 1 < len(spans):
             wait_span(keys, k_buf, k_sem, g + 1)
@@ -238,26 +246,21 @@
             wait_span(values, v_buf, v_sem, g)
         weigh(g, parts)
 
-        @pl.when(core != PAIR - 1)
-        def _():
-            if g == 0:
-                pl.semaphore_wait(barrier, n_chip)
-                pl.semaphore_signal(
-                    ring_sem, inc=1, device_id={"seq": me + 1}, device_id_type=MESH
-                )
-            for e in span:
-                to_owner(e).start()
-
-        if g >= ready:
+        if g == 0:
 
             @pl.when(core == PAIR - 1)
             def _():
-                if g == ready:
-                    pl.semaphore_wait(ring_sem, 1)
-                done = order[: (ready + 1) * SPAN] if g == ready else span
-                for e in far:
-                    if e in done:
-                        to_owner(e).start()
+                pl.semaphore_wait(barrier, n_chip + n_head - 1)
+                tell_partner()
+
+            @pl.when(core != PAIR - 1)
+            def _():
+                pl.semaphore_wait(told, 1)
+                to_owner(0).start()
+
+        for e in span:
+            if e:
+                to_owner(e).start()
 
     for load in late:
         load.wait()
@@ -302,6 +305,8 @@
 
     @pl.when(core != PAIR - 1)
     def _():
+        pl.semaphore_wait(barrier, n_head - 1)
+        tell_partner()
         arrived(recv2, recv_sem2)
         finish()
         gone(send1, send_sem1)
@@ -348,8 +353,11 @@
             for c in range(PAIR):
                 send2[h * PAIR + c, 0:cands, :] = part[c * cands : (c + 1) * cands]
                 send2[h * PAIR + c, cands : cands + 1, :] = squares[c]
-        pl.semaphore_wait(barrier, PAIR * (n_head - 1))
-        for e in far_first(n_head)[:-1]:
+        heads = far_first(n_head)[:-1]
+        across(heads[0], PAIR - 1).start()
+        pl.semaphore_wait(told, 1)
+        across(heads[0], 0).start()
+        for e in heads[1:]:
             for c in range(PAIR):
                 across(e, c).start()
         across(0, 0).start()

time: 28.2 us -> 27.7 us (0.982)
  Pallas kernels: 27.5 us -> 27 us
    pallas_call x1, Pallas kernels: 27.5 us -> 27 us  [body(): pl.pallas_call(kernel, name='decode', out_shape=pltpu.VMEM((users // n_se...]
where the time goes in v5:
time: 27.7 us; the launch traced here: 27.6 us
  Pallas kernels  27 us (97%)
  local copies, waits for them, and re-layouts  0.6 us (2%)
    pallas_call x1, Pallas kernels, body(): pl.pallas_call(kernel, name='decode', out_shape=pltpu.VMEM((users // n_se...  27 us
    unnamed x1, local copies, waits for them, and re-layouts  0.6 us

profile of v5, /device:TPU:513, one launch (start us, length us, event | category | flops | bytes accessed | tf_op | source)
XLA Modules:
  0.0 27.6 jit_solution(10242249403060828226)
XLA Ops:
  0.0 27.0 %decode.1 = bf16[1,16,128]{2,1,0:T(8,128)(2,1)S(1)} custom-call(bf16[16,16,128]{2,1,0:T(8,128)(2,1)} %query.1, bf16[16,16,128]{2,1,0:T(8,128)(2,1)} %new_key.1, bf16[16,16,128]{2,1,0:T(8,128)(2,1)} %new_value.1, bf16[16,1024,128]{2,1,0:T(8,128)(2,1)} %keys.1, bf16[16,1024,128]{2,1,0:T(8,128)(2,1)} %values.1, s32[16]{0:T(128)} %lengths.1, ...), custom_call_target="tpu_custom_call" | custom-call | tf_op jit(solution)/shard_map/decode/pallas_call | solution.py:396
  27.0 0.6 %copy.15 = bf16[1,16,128]{2,1,0:T(8,128)(2,1)} copy(bf16[1,16,128]{2,1,0:T(8,128)(2,1)S(1)} %decode.1) | data formatting | bytes 8192

commit v6 on v5

--- a/solution.py
+++ b/solution.py
@@ -68,6 +68,7 @@
     send_sem2,
     recv_sem2,
     told,
+    across_in,
 ):
     n_seq = lax.axis_size("seq")
     n_head = lax.axis_size("head")
@@ -80,7 +81,7 @@
     pair_rows = PAIR * cands
     scale = LOG2E / math.sqrt(width)
     far = far_first(n_chip)[:-1]
-    order = [0, far[0], 1] + [e for e in far[1:] if e != 1]
+    order = list(range(n_chip))
     f32, bf16 = jnp.float32, jnp.bfloat16
 
     def chip_at(e):
@@ -126,6 +127,34 @@
     start_span(keys, k_buf, k_sem, 0)
     for load in early[1:]:
         load.start()
+    barrier = pltpu.get_barrier_semaphore()
+    half = n_chip // 2
+    in_last = lax.div(chip, half)
+    partner = chip * PAIR + PAIR - 1 - core
+
+    def to_last(e):
+        return chip_at(e) >= half
+
+    pl.semaphore_signal(barrier, inc=1, device_id={"seq": partner}, device_id_type=MESH)
+
+    @pl.when(core == PAIR - 1)
+    def _():
+        for e in far:
+            pl.semaphore_signal(
+                barrier,
+                inc=1,
+                device_id={"seq": chip_at(e) * PAIR + in_last},
+                device_id_type=MESH,
+            )
+
+        for e in far_first(n_head)[:-1]:
+            pl.semaphore_signal(
+                barrier,
+                inc=1,
+                device_id={"seq": partner, "head": head_at(e)},
+                device_id_type=MESH,
+            )
+
     for g in range(1, len(spans)):
         start_span(keys, k_buf, k_sem, g)
         start_span(values, v_buf, v_sem, g - 1)
@@ -133,31 +162,20 @@
     for load in late:
         load.start()
 
-    barrier = pltpu.get_barrier_semaphore()
-
-    @pl.when(core == PAIR - 1)
+    def tell_partner():
+        pl.semaphore_signal(told, inc=1, device_id={"seq": partner}, device_id_type=MESH)
+
+    @pl.when(core != PAIR - 1)
     def _():
-        for e in far:
+        pl.semaphore_wait(barrier, n_head + half - 1 + in_last)
+        tell_partner()
+        for e in far_first(n_head)[:-1]:
             pl.semaphore_signal(
-                barrier,
+                across_in,
                 inc=1,
-                device_id={"seq": chip_at(e) * PAIR + PAIR - 1},
+                device_id={"seq": partner, "head": head_at(e)},
                 device_id_type=MESH,
             )
-
-    @pl.when(core != PAIR - 1)
-    def _():
-        pl.semaphore_signal(
-            barrier, inc=1, device_id={"seq": chip * PAIR + PAIR - 1}, device_id_type=MESH
-        )
-
-    for e in far_first(n_head)[:-1]:
-        pl.semaphore_signal(barrier, inc=1, device_id={"head": head_at(e)}, device_id_type=MESH)
-
-    def tell_partner():
-        pl.semaphore_signal(
-            told, inc=1, device_id={"seq": chip * PAIR + PAIR - 1 - core}, device_id_type=MESH
-        )
 
     diag = lax.broadcasted_iota(jnp.int32, (cands, LANES), 1) - lax.broadcasted_iota(
         jnp.int32, (cands, LANES), 0
@@ -250,17 +268,36 @@
 
             @pl.when(core == PAIR - 1)
             def _():
-                pl.semaphore_wait(barrier, n_chip + n_head - 1)
-                tell_partner()
+                pl.semaphore_wait(told, 1)
 
             @pl.when(core != PAIR - 1)
             def _():
-                pl.semaphore_wait(told, 1)
                 to_owner(0).start()
 
         for e in span:
             if e:
+
+                @pl.when(jnp.logical_not(to_last(e)))
+                def _():
+                    to_owner(e).start()
+
+    def send_last():
+        for e in far:
+
+            @pl.when(to_last(e))
+            def _():
                 to_owner(e).start()
+
+    @pl.when(core != PAIR - 1)
+    def _():
+        pl.semaphore_wait(told, 1)
+        send_last()
+
+    @pl.when(core == PAIR - 1)
+    def _():
+        pl.semaphore_wait(barrier, 1 + half - in_last)
+        tell_partner()
+        send_last()
 
     for load in late:
         load.wait()
@@ -305,8 +342,6 @@
 
     @pl.when(core != PAIR - 1)
     def _():
-        pl.semaphore_wait(barrier, n_head - 1)
-        tell_partner()
         arrived(recv2, recv_sem2)
         finish()
         gone(send1, send_sem1)
@@ -354,13 +389,13 @@
                 send2[h * PAIR + c, 0:cands, :] = part[c * cands : (c + 1) * cands]
                 send2[h * PAIR + c, cands : cands + 1, :] = squares[c]
         heads = far_first(n_head)[:-1]
-        across(heads[0], PAIR - 1).start()
-        pl.semaphore_wait(told, 1)
-        across(heads[0], 0).start()
-        for e in heads[1:]:
-            for c in range(PAIR):
-                across(e, c).start()
+        for e in heads:
+            across(e, PAIR - 1).start()
+
         across(0, 0).start()
+        pl.semaphore_wait(across_in, n_head - 1)
+        for e in heads:
+            across(e, 0).start()
         recv2[0] = send2[my_head * PAIR + PAIR - 1]
         arrived(recv2.at[pl.ds(1, n_head - 1)], recv_sem2)
         finish()
@@ -387,7 +422,7 @@
     cands = query.shape[1]
     n_seq, n_head = lax.axis_size("seq"), lax.axis_size("head")
     assert users == n_seq and width == LANES and w_out.shape[1] == n_head * width
-    assert n_seq % (PAIR * SPAN) == 0 and 4 * cands <= LANES
+    assert n_seq % (2 * PAIR * SPAN) == 0 and 4 * cands <= LANES
     n_chip = n_seq // PAIR
     tile = PAIR * cands + 1
     bf16, f32, i32 = jnp.bfloat16, jnp.float32, jnp.int32
@@ -427,6 +462,7 @@
             dma,
             dma,
             pltpu.SemaphoreType.REGULAR,
+            pltpu.SemaphoreType.REGULAR,
         ],
         compiler_params=pltpu.CompilerParams(collective_id=0, has_side_effects=True),
     )(

time: 27.7 us -> 26.3 us (0.949)
  Pallas kernels: 27 us -> 25.7 us
    pallas_call x1, Pallas kernels: 27 us -> 25.7 us  [body(): pl.pallas_call(kernel, name='decode', out_shape=pltpu.VMEM((users // n_se...]
where the time goes in v6:
time: 26.3 us
  Pallas kernels  25.7 us (98%)
  local copies, waits for them, and re-layouts  0.6 us (2%)
    pallas_call x1, Pallas kernels, body(): pl.pallas_call(kernel, name='decode', out_shape=pltpu.VMEM((users // n_se...  25.7 us
    unnamed x1, local copies, waits for them, and re-layouts  0.6 us

profile of v6, /device:TPU:513, one launch (start us, length us, event | category | flops | bytes accessed | tf_op | source)
XLA Modules:
  0.0 26.3 jit_solution(5667027820875575566)
XLA Ops:
  0.0 25.7 %decode.1 = bf16[1,16,128]{2,1,0:T(8,128)(2,1)S(1)} custom-call(bf16[16,16,128]{2,1,0:T(8,128)(2,1)} %query.1, bf16[16,16,128]{2,1,0:T(8,128)(2,1)} %new_key.1, bf16[16,16,128]{2,1,0:T(8,128)(2,1)} %new_value.1, bf16[16,1024,128]{2,1,0:T(8,128)(2,1)} %keys.1, bf16[16,1024,128]{2,1,0:T(8,128)(2,1)} %values.1, s32[16]{0:T(128)} %lengths.1, ...), custom_call_target="tpu_custom_call" | custom-call | tf_op jit(solution)/shard_map/decode/pallas_call | solution.py:431
  25.7 0.6 %copy.15 = bf16[1,16,128]{2,1,0:T(8,128)(2,1)} copy(bf16[1,16,128]{2,1,0:T(8,128)(2,1)S(1)} %decode.1) | data formatting | bytes 8192

commit v7 on v6

--- a/solution.py
+++ b/solution.py
@@ -16,6 +16,18 @@
 
 def far_first(count):
     return sorted(range(count), key=lambda d: (-min(d, count - d), d))
+
+
+def spans_of(order):
+    order = list(order)
+    return [order[:1], order[1:2]] + [order[i : i + SPAN] for i in range(2, len(order), SPAN)]
+
+
+def tree_sum(terms):
+    while len(terms) > 1:
+        pairs = [a + b for a, b in zip(terms[::2], terms[1::2])]
+        terms = pairs + terms[len(pairs) * 2 :]
+    return terms[0]
 
 
 def lane_table(table):
@@ -81,7 +93,7 @@
     pair_rows = PAIR * cands
     scale = LOG2E / math.sqrt(width)
     far = far_first(n_chip)[:-1]
-    order = list(range(n_chip))
+    order = sorted(range(n_chip), key=lambda e: (e + 1.5 if e == 3 else e))
     f32, bf16 = jnp.float32, jnp.bfloat16
 
     def chip_at(e):
@@ -112,16 +124,20 @@
         pltpu.make_async_copy(src, dst, in_sem.at[i]) for i, (src, dst) in enumerate(early + late)
     ]
     early, late = loads[: len(early)], loads[len(early) :]
-    spans = [order[i : i + SPAN] for i in range(0, n_chip, SPAN)]
+    spans = spans_of(order)
+    places = {e: i * PAIR for i, e in enumerate(order)}
 
     def start_span(source, buf, sem, g):
-        for i, e in enumerate(spans[g]):
+        for e in spans[g]:
             pltpu.make_async_copy(
-                pair_of(source, e), buf.at[g, pl.ds(i * PAIR, PAIR)], sem.at[g]
+                pair_of(source, e), buf.at[pl.ds(places[e], PAIR)], sem.at[g]
             ).start()
 
     def wait_span(source, buf, sem, g):
-        pltpu.make_async_copy(source.at[pl.ds(0, SPAN * PAIR)], buf.at[g], sem.at[g]).wait()
+        count = len(spans[g]) * PAIR
+        pltpu.make_async_copy(
+            source.at[pl.ds(0, count)], buf.at[pl.ds(places[spans[g][0]], count)], sem.at[g]
+        ).wait()
 
     early[0].start()
     start_span(keys, k_buf, k_sem, 0)
@@ -171,7 +187,7 @@
         tell_partner()
         for e in far_first(n_head)[:-1]:
             pl.semaphore_signal(
-                across_in,
+                across_in.at[n_head - e],
                 inc=1,
                 device_id={"seq": partner, "head": head_at(e)},
                 device_id_type=MESH,
@@ -192,11 +208,11 @@
         return jnp.sum(picked, axis=1, keepdims=True)
 
     def score(g):
-        for i, e in enumerate(spans[g]):
+        for e in spans[g]:
             for c in range(PAIR):
                 score_buf[e, c] = lax.dot_general(
                     q_buf[chip_at(e) * PAIR + c],
-                    k_buf[g, i * PAIR + c],
+                    k_buf[places[e] + c],
                     (((1,), (1,)), ((), ())),
                     preferred_element_type=f32,
                 )
@@ -217,10 +233,10 @@
         return parts
 
     def weigh(g, parts):
-        for i, e in enumerate(spans[g]):
+        for e in spans[g]:
             for c in range(PAIR):
                 send1[e, c * cands : (c + 1) * cands, :] = jnp.dot(
-                    parts[e, c], v_buf[g, i * PAIR + c], preferred_element_type=f32
+                    parts[e, c], v_buf[places[e] + c], preferred_element_type=f32
                 )
 
     def to_owner(e):
@@ -333,9 +349,7 @@
         ).wait_send()
 
     def finish():
-        whole = recv2[0]
-        for e in range(1, n_head):
-            whole = whole + recv2[e]
+        whole = tree_sum([recv2[e] for e in range(n_head)])
         square_sum = as_column(whole[cands : cands + 1], 0)
         factor = 1.0 / jnp.sqrt(square_sum / (width * n_head) + 1e-06)
         out[0] = (whole[:cands] * factor).astype(out.dtype)
@@ -372,12 +386,11 @@
         denom = own_factor + jnp.sum(factors * totals, axis=0, keepdims=True)
         hidden, squares = [], {}
         for c in range(PAIR):
-            numer = as_column(own_factor, 2 * c) * own_value[c]
+            terms = [as_column(own_factor, 2 * c) * own_value[c]]
             for i, slot in enumerate(slots):
-                numer = numer + as_column(factors[i : i + 1], 2 * c) * slot[
-                    c * cands : (c + 1) * cands, :
-                ]
-            attended = numer / as_column(denom, 2 * c)
+                rows = slot[c * cands : (c + 1) * cands, :]
+                terms.append(as_column(factors[i : i + 1], 2 * c) * rows)
+            attended = tree_sum(terms) / as_column(denom, 2 * c)
             squares[c] = as_row({0: jnp.sum(attended * attended, axis=1, keepdims=True)})
             hidden.append((attended * gated[c]).astype(bf16))
         hidden = jnp.concatenate(hidden, axis=0)
@@ -389,13 +402,18 @@
                 send2[h * PAIR + c, 0:cands, :] = part[c * cands : (c + 1) * cands]
                 send2[h * PAIR + c, cands : cands + 1, :] = squares[c]
         heads = far_first(n_head)[:-1]
+        heads = [heads[0]] + sorted(heads[1:], key=lambda e: e != 1)
+        for e in heads[:2]:
+            across(e, PAIR - 1).start()
+        pl.semaphore_wait(across_in.at[1], 1)
+        across(1, 0).start()
+        for e in heads[2:]:
+            across(e, PAIR - 1).start()
+        across(0, 0).start()
         for e in heads:
-            across(e, PAIR - 1).start()
-
-        across(0, 0).start()
-        pl.semaphore_wait(across_in, n_head - 1)
-        for e in heads:
-            across(e, 0).start()
+            if e != 1:
+                pl.semaphore_wait(across_in.at[e], 1)
+                across(e, 0).start()
         recv2[0] = send2[my_head * PAIR + PAIR - 1]
         arrived(recv2.at[pl.ds(1, n_head - 1)], recv_sem2)
         finish()
@@ -438,8 +456,8 @@
             vmem((users, cands, width), bf16),
             vmem((PAIR, cands, width), bf16),
             vmem((PAIR, cands, width), bf16),
-            vmem((n_chip // SPAN, SPAN * PAIR, block_len, width), bf16),
-            vmem((n_chip // SPAN, SPAN * PAIR, block_len, width), bf16),
+            vmem((users, block_len, width), bf16),
+            vmem((users, block_len, width), bf16),
             pltpu.SMEM((users,), i32),
             vmem((users, block_len), i32),
             vmem((users, block_len), i32),
@@ -455,14 +473,14 @@
             vmem((n_head * PAIR, cands + 1, width), f32),
             vmem((n_head, cands + 1, width), f32),
             dma((11,)),
-            dma((n_chip // SPAN,)),
-            dma((n_chip // SPAN,)),
+            dma((len(spans_of(range(n_chip))),)),
+            dma((len(spans_of(range(n_chip))),)),
             dma,
             dma,
             dma,
             dma,
             pltpu.SemaphoreType.REGULAR,
-            pltpu.SemaphoreType.REGULAR,
+            pltpu.SemaphoreType.REGULAR((n_head,)),
         ],
         compiler_params=pltpu.CompilerParams(collective_id=0, has_side_effects=True),
     )(

time: 26.3 us -> 26.2 us (level)
  no operation moved by 1% of the time
where the time goes in v7:
time: 26.2 us; the launch traced here: 26.1 us
  Pallas kernels  25.5 us (97%)
  local copies, waits for them, and re-layouts  0.6 us (2%)
    pallas_call x1, Pallas kernels, body(): pl.pallas_call(kernel, name='decode', out_shape=pltpu.VMEM((users // n_se...  25.5 us
    unnamed x1, local copies, waits for them, and re-layouts  0.6 us

profile of v7, /device:TPU:513, one launch (start us, length us, event | category | flops | bytes accessed | tf_op | source)
XLA Modules:
  0.0 26.1 jit_solution(207861847337546830)
XLA Ops:
  0.0 25.5 %decode.1 = bf16[1,16,128]{2,1,0:T(8,128)(2,1)S(1)} custom-call(bf16[16,16,128]{2,1,0:T(8,128)(2,1)} %query.1, bf16[16,16,128]{2,1,0:T(8,128)(2,1)} %new_key.1, bf16[16,16,128]{2,1,0:T(8,128)(2,1)} %new_value.1, bf16[16,1024,128]{2,1,0:T(8,128)(2,1)} %keys.1, bf16[16,1024,128]{2,1,0:T(8,128)(2,1)} %values.1, s32[16]{0:T(128)} %lengths.1, ...), custom_call_target="tpu_custom_call" | custom-call | tf_op jit(solution)/shard_map/decode/pallas_call | solution.py:449
  25.5 0.6 %copy.15 = bf16[1,16,128]{2,1,0:T(8,128)(2,1)} copy(bf16[1,16,128]{2,1,0:T(8,128)(2,1)S(1)} %decode.1) | data formatting | bytes 8192
